TPU v7x, 512 devices: a whole 4x4x16 slice. The times are simulated.
512 devices in a mesh: dp: 4 (over y), tensor: 8 (over z_hi, x), enc: 16 (over z_lo, core).
Axes of the slice: x: 4, y: 4, z: 16 (z_hi: 2, z_lo: 8; z = z_hi * 8 + z_lo), core: 2. Of those that a mesh axis runs over, the one named last changes fastest.
Arguments:
- span_states: bfloat16 [8192, 8192], P(('dp', 'enc'), 'tensor'), may hold values from -6 to 6
- neighbours: bfloat16 [128, 256, 1024], P(('dp', 'enc'), None, 'tensor'), may hold values from -6 to 6
- lengths: int32 [4], P('dp'), may hold values from 1 to 2048, 4096 in all
- wq_enc: bfloat16 [1024, 1024], P('enc', 'tensor')
- wk_enc: bfloat16 [8192, 1024], P('enc', 'tensor'), may hold values from -0.0625 to 0.0625
- wv_enc: bfloat16 [8192, 1024], P('enc', 'tensor'), may hold values from -0.0625 to 0.0625
- wo_enc: bfloat16 [1024, 1024], P('enc', 'tensor'), may hold values from -0.1875 to 0.1875
- wk_dec: bfloat16 [1024, 8192], P(('dp', 'enc'), 'tensor'), may hold values from -0.1875 to 0.1875
- wv_dec: bfloat16 [1024, 8192], P(('dp', 'enc'), 'tensor'), may hold values from -0.1875 to 0.1875
- queries: bfloat16 [8192, 8192], P(('dp', 'enc'), 'tensor'), may hold values from -6 to 6
- grad_out: bfloat16 [8192, 8192], P(('dp', 'enc'), 'tensor'), may hold values from -6 to 6
Outputs:
- attended: bfloat16 [8192, 8192], P(('dp', 'enc'), 'tensor')
- grad_encoded: float32 [128, 256, 1024], P(('dp', 'enc'), None, 'tensor')
Inputs may be any that keep to these rules, and one draw needn't show every extreme that they name: `lengths`: some sequence is live over all 2048 tokens.
All inputs are finite; a program needn't handle non-finite values. No bound on the sum of `lengths` on one device may be relied on, other than what follows from the above.
Results may differ from a plain program's by a relative error of at most 0.019.
Values may be sent and summed in bfloat16 or wider, within the bound.
A program may use at most 64 MiB of HBM per device.

v0:
```python
import math

import jax
import jax.numpy as jnp
from jax import lax
from jax.sharding import Mesh
from jax.sharding import PartitionSpec as P

HD = 128
EH = 64
TENSOR = ("tensor_0", "tensor_1")


def in_order(blocks, dim):
    dims = list(blocks.shape[1:])
    dims[dim] *= blocks.shape[0]
    return jnp.moveaxis(blocks, 0, dim).reshape(dims)


def one_gather(arrays, axis, dims):
    vector = jnp.concatenate([a.reshape(-1) for a in arrays])
    lines, at, gathered = (lax.all_gather(vector, axis), 0, [])
    for a, dim in zip(arrays, dims):
        blocks = lines[:, at : at + a.size].reshape(-1, *a.shape)
        gathered.append(in_order(blocks, dim))
        at += a.size
    return tuple(gathered)


def copy_for_each(x, axis):
    copies = jnp.broadcast_to(x, (lax.axis_size(axis), *x.shape))
    return lax.all_to_all(copies, axis, split_axis=0, concat_axis=0, tiled=True)


def gathered_copies(x, axis, dim):
    blocks = copy_for_each(x, axis)
    return in_order(blocks, dim)


def in_one_piece(arrays, axis, dim, along):
    both = jnp.concatenate(arrays, axis=along)
    filled, at, gathered = (lax.all_gather(both, axis, axis=dim, tiled=True), 0, [])
    for a in arrays:
        gathered.append(lax.slice_in_dim(filled, at, at + a.shape[along], axis=along))
        at += a.shape[along]
    return tuple(gathered)


def from_behind(value, axis, steps):
    count = lax.axis_size(axis)
    first, last = (max(0, -steps), min(count, count - steps))
    return lax.ppermute(value, axis, [(source, source + steps) for source in range(first, last)])


def sum_in_order(blocks, axes, turns):
    inside = blocks.shape[1:]
    blocks = blocks.reshape(*(lax.axis_size(a) for a in axes), *inside)
    blocks = jnp.moveaxis(blocks, turns, range(len(axes))).reshape(-1, *inside)
    for k in turns:
        blocks = lax.psum_scatter(blocks, axes[k], scatter_dimension=0, tiled=True)
    return blocks[0]


def in_blocks(x, dim, count):
    before, after = (x.shape[:dim], x.shape[dim + 1 :])
    return jnp.moveaxis(x.reshape(*before, count, -1, *after), dim, 0)


def summed_rows(x, axes, turns, dim):
    count = lax.axis_size(axes)
    return sum_in_order(in_blocks(x, dim, count), axes, turns)


def on_device(
    span_states,
    neighbours,
    lengths,
    wq_enc,
    wk_enc,
    wv_enc,
    wo_enc,
    wk_dec,
    wv_dec,
    queries,
    grad_out,
):
    spans, keys_each, width = neighbours.shape
    row_count = span_states.shape[0]
    span_len = row_count // spans
    key_rows = spans * keys_each
    flat_neighbour = neighbours.reshape(key_rows, width)
    full_states, full_neighbour = one_gather((span_states, flat_neighbour), TENSOR, (1, 1))
    sliced = full_neighbour
    query_sum = jnp.dot(
        sliced, gathered_copies(wq_enc, "enc", 0), preferred_element_type=jnp.float32
    )
    segments = in_one_piece((wk_enc, wv_enc), "enc", 0, 1)
    sliced = full_states
    key_sum = jnp.dot(sliced, segments[0], preferred_element_type=jnp.float32)
    value_sum = jnp.dot(sliced, segments[1], preferred_element_type=jnp.float32)
    heads_enc = width // EH
    query_heads = query_sum.astype(jnp.bfloat16).reshape(spans, keys_each, heads_enc, EH)
    key_heads = key_sum.astype(jnp.bfloat16).reshape(spans, span_len, heads_enc, EH)
    value_heads = value_sum.astype(jnp.bfloat16).reshape(spans, span_len, heads_enc, EH)
    scores = jnp.einsum(
        "cqhe,ckhe->chqk", query_heads, key_heads, preferred_element_type=jnp.float32
    ) / math.sqrt(EH)
    enc_weights = jax.nn.softmax(scores, axis=-1).astype(jnp.bfloat16)
    head_mix = jnp.einsum(
        "chqk,ckhe->cqhe", enc_weights, value_heads, preferred_element_type=jnp.float32
    )
    head_mix = head_mix.astype(jnp.bfloat16).reshape(key_rows, width)
    full_mix = lax.all_gather(head_mix, TENSOR, axis=1, tiled=True)
    sliced = full_mix
    output_sum = jnp.dot(
        sliced, gathered_copies(wo_enc, "enc", 0), preferred_element_type=jnp.float32
    )
    encoded = (
        (flat_neighbour.astype(jnp.float32) + output_sum)
        .astype(jnp.bfloat16)
        .reshape(spans, keys_each, width)
    )
    carried = from_behind(encoded[spans - 1], "enc", 1)
    previous_part = jnp.concatenate([carried[None], encoded[: spans - 1]], axis=0).reshape(
        key_rows, width
    )
    previous = lax.all_gather(previous_part, TENSOR, axis=1, tiled=True)
    key_weight, value_weight = in_one_piece((wk_dec, wv_dec), ("dp", "enc"), 0, 1)
    dec_key = jnp.dot(previous, key_weight, preferred_element_type=jnp.float32).astype(jnp.bfloat16)
    dec_value = jnp.dot(previous, value_weight, preferred_element_type=jnp.float32).astype(
        jnp.bfloat16
    )
    heads_dec = queries.shape[1] // HD
    query_dec = queries.reshape(spans, span_len, heads_dec, HD)
    key_dec = dec_key.reshape(spans, keys_each, heads_dec, HD)
    value_dec = dec_value.reshape(spans, keys_each, heads_dec, HD)
    dec_scores = jnp.einsum(
        "cmhd,ckhd->chmk", query_dec, key_dec, preferred_element_type=jnp.float32
    ) / math.sqrt(HD)
    probs = jax.nn.softmax(dec_scores, axis=-1)
    probs_low = probs.astype(jnp.bfloat16)
    position = lax.axis_index("enc") * row_count + jnp.arange(row_count, dtype=jnp.int32)
    live_mask = jnp.logical_and(position < lengths[0], position >= span_len).reshape(
        spans, span_len, 1, 1
    )
    attended = jnp.einsum(
        "chmk,ckhd->cmhd", probs_low, value_dec, preferred_element_type=jnp.float32
    )
    attended = jnp.where(live_mask, attended, 0.0).astype(jnp.bfloat16).reshape(row_count, -1)
    cotangent = jnp.where(
        live_mask, grad_out.reshape(spans, span_len, heads_dec, HD), jnp.zeros((), jnp.bfloat16)
    )
    grad_value = jnp.einsum(
        "chmk,cmhd->ckhd", probs_low, cotangent, preferred_element_type=jnp.float32
    ).astype(jnp.bfloat16)
    grad_probs = jnp.einsum(
        "cmhd,ckhd->chmk", cotangent, value_dec, preferred_element_type=jnp.float32
    )
    inner = jnp.sum(grad_probs * probs, axis=-1, keepdims=True)
    grad_scores = (probs * (grad_probs - inner) / math.sqrt(HD)).astype(jnp.bfloat16)
    grad_key = jnp.einsum(
        "chmk,cmhd->ckhd", grad_scores, query_dec, preferred_element_type=jnp.float32
    ).astype(jnp.bfloat16)
    partial_value = jnp.einsum(
        "nd,ed->ne", grad_key.reshape(key_rows, -1), key_weight, preferred_element_type=jnp.float32
    )
    partial_value = partial_value + jnp.einsum(
        "nd,ed->ne",
        grad_value.reshape(key_rows, -1),
        value_weight,
        preferred_element_type=jnp.float32,
    )
    returned = (
        summed_rows(partial_value.astype(jnp.bfloat16), TENSOR, (1, 0), 1)
        .astype(jnp.float32)
        .reshape(spans, keys_each, width)
    )
    following = from_behind(returned[0].astype(jnp.bfloat16), "enc", -1).astype(jnp.float32)
    grad_encoded = jnp.concatenate([returned[1:], following[None]], axis=0)
    return (attended, grad_encoded)


def solution(mesh):
    split = Mesh(
        mesh.devices.reshape(mesh.shape["dp"], 2, 4, mesh.shape["enc"]),
        ("dp", "tensor_0", "tensor_1", "enc"),
    )
    in_specs = (
        P(("dp", "enc"), TENSOR),
        P(("dp", "enc"), None, TENSOR),
        P("dp"),
        P("enc", TENSOR),
        P("enc", TENSOR),
        P("enc", TENSOR),
        P("enc", TENSOR),
        P(("dp", "enc"), TENSOR),
        P(("dp", "enc"), TENSOR),
        P(("dp", "enc"), TENSOR),
        P(("dp", "enc"), TENSOR),
    )
    out_specs = (P(("dp", "enc"), TENSOR), P(("dp", "enc"), None, TENSOR))
    return jax.shard_map(
        on_device, mesh=split, in_specs=in_specs, out_specs=out_specs, check_vma=False
    )
```

profile of v0, /device:TPU:1, one launch (start us, length us, event | category | flops | bytes accessed | tf_op | source)
XLA Modules:
  0.0 678.9 jit_solution(7648377399311561809)
XLA Ops:
  12.5 14.0 %all-to-all-start = ((bf16[16,64,128]{2,1,0:T(8,128)(2,1)}), bf16[16,64,128]{2,1,0:T(8,128)(2,1)S(1)}, u32[]{:S(2)}, u32[]{:S(2)}) async-start(bf16[16,64,128]{2,1,0:T(8,128)(2,1)} %broadcast_in_dim.43), calls=%async_computation | async-start | bytes 524288 | tf_op jit(solution)/shard_map/all_to_all | solution.py:32
  26.5 135.1 %all-gather.15.cloned.1.call-done = bf16[1572864]{0:T(1024)(128)(2,1)} async-done(((bf16[196608]{0:T(1024)(128)(2,1)}), bf16[1572864]{0:T(1024)(128)(2,1)}) %all-gather.15.cloned.1.call-update) | async-done | bytes 3145744 | tf_op jit(solution)/shard_map/all_gather | solution.py:22
  161.7 3.2 reshape.126
  166.9 1.8 convolution_convert_fusion.3
  168.9 2.7 copy.56
  171.6 93.4 %all-gather.7.cloned.1.call-done = bf16[8192,256]{1,0:T(8,128)(2,1)} async-done(((bf16[512,256]{1,0:T(8,128)(2,1)}), bf16[8192,256]{1,0:T(8,128)(2,1)}) %all-gather.7.cloned.1.call-update) | async-done | bytes 4194320 | tf_op jit(solution)/shard_map/all_gather | solution.py:42
  265.0 3.1 fusion.50
  268.5 2.3 fusion.47
  272.8 27.9 %all_to_all.10 = bf16[16,64,128]{2,1,0:T(8,128)(2,1)S(1)} all-to-all(bf16[16,64,128]{2,1,0:T(8,128)(2,1)S(1)} %broadcast_in_dim.44), channel_id=1, replica_groups=mesh['dp'=4,'tensor_0'=2,'tensor_1'=4,'enc'=16] {'enc'}, dimensions={0} | all-to-all | bytes 524288 | tf_op jit(solution)/shard_map/all_to_all | solution.py:32
  300.8 63.7 %all-gather.9.cloned.1.call-done = bf16[512,1024]{0,1:T(8,128)(2,1)} async-done(((bf16[512,128]{0,1:T(8,128)(2,1)}), bf16[512,1024]{0,1:T(8,128)(2,1)}) %all-gather.9.cloned.1.call-update) | async-done | bytes 1048592 | tf_op jit(solution)/shard_map/all_gather | solution.py:113
  366.2 1.9 collective-permute-start
  368.1 2.3 collective-permute-done
  372.2 109.5 %all-gather.13.cloned.1.call-done = bf16[1024,2048]{1,0:T(8,128)(2,1)} async-done(((bf16[16,2048]{1,0:T(8,128)(2,1)}), bf16[1024,2048]{1,0:T(8,128)(2,1)}) %all-gather.13.cloned.1.call-update) | async-done | bytes 4194320 | tf_op jit(solution)/shard_map/all_gather | solution.py:42
  481.6 85.6 %all-gather.11.cloned.1.call-done = bf16[512,1024]{1,0:T(8,128)(2,1)} async-done(((bf16[512,128]{1,0:T(8,128)(2,1)}), bf16[512,1024]{1,0:T(8,128)(2,1)}) %all-gather.11.cloned.1.call-update) | async-done | bytes 1048592 | tf_op jit(solution)/shard_map/all_gather | solution.py:127
  567.2 3.3 fusion.27
  575.0 3.2 fusion.25
  578.1 2.4 copy.51
  582.1 8.7 %fusion.24 = bf16[2,256,8,128]{3,1,2,0:T(8,128)(2,1)} fusion(f32[2,8,64,256]{3,2,1,0:T(8,128)S(1)} %fusion.62, bf16[2,64,8,128]{3,2,1,0:T(8,128)(2,1)S(1)} %bitcast.103, f32[2,8,64,256]{3,2,1,0:T(8,128)} %get-tuple-element.7, f32[2,8,64]{2,1,0:T(8,128)S(1)} %get-tuple-element.6), kind=kOutput, calls=%fused_computation.21 | convolution fusion | flops 69469440 | bytes 3411968 | tf_op jit(solution)/shard_map/chmk,cmhd->ckhd/dot_general | solution.py:161
  590.8 2.0 copy.50
  592.8 3.0 fusion.7
  598.7 22.4 %reduce-scatter.3.cloned.1.call-done = bf16[2,512,128]{2,1,0:T(8,128)(2,1)} async-done(((bf16[8,512,128]{2,1,0:T(8,128)(2,1)}), bf16[2,512,128]{2,1,0:T(8,128)(2,1)}) %reduce-scatter.3.cloned.1.call-update) | async-done | bytes 262160 | tf_op jit(solution)/shard_map/reduce_scatter | solution.py:60
  621.1 43.8 %reduce-scatter.5.cloned.1.call-done = bf16[1,512,128]{2,1,0:T(8,128)(2,1)} async-done(((bf16[2,512,128]{2,1,0:T(8,128)(2,1)}), bf16[1,512,128]{2,1,0:T(8,128)(2,1)}) %reduce-scatter.5.cloned.1.call-update) | async-done | bytes 131088 | tf_op jit(solution)/shard_map/reduce_scatter | solution.py:60
  665.8 2.6 collective-permute-start.1
  668.4 1.9 fusion.43
  (80 shorter events, 23.8 us)
Async XLA Ops:
  7.2 4.5 copy-start.9
  7.2 154.5 %all-gather.15.cloned.1.call-start = ((), (), s32[]{:S(2)}) async-start(), calls=%async_computation.10 | async-start | bytes 3538944 | tf_op jit(solution)/shard_map/all_gather | solution.py:22
  9.9 255.1 %all-gather.7.cloned.1.call-start = ((), (), s32[]{:S(2)}) async-start(), calls=%async_computation.4 | async-start | bytes 4456448 | tf_op jit(solution)/shard_map/all_gather | solution.py:42
  12.5 154.4 %all-to-all-start = ((bf16[16,64,128]{2,1,0:T(8,128)(2,1)}), bf16[16,64,128]{2,1,0:T(8,128)(2,1)S(1)}, u32[]{:S(2)}, u32[]{:S(2)}) async-start(bf16[16,64,128]{2,1,0:T(8,128)(2,1)} %broadcast_in_dim.43), calls=%async_computation | async-start | bytes 524288 | tf_op jit(solution)/shard_map/all_to_all | solution.py:32
  26.5 338.0 %all-gather.9.cloned.1.call-start = ((), (), s32[]{:S(2)}) async-start(), calls=%async_computation.5 | async-start | bytes 1179648 | tf_op jit(solution)/shard_map/all_gather | solution.py:113
  164.9 2.0 copy-start
  166.9 2.0 slice-start
  265.0 3.5 copy-start.1
  268.5 3.6 copy-start.7
  268.5 3.6 copy-start.8
  270.8 2.0 copy-start.10
  270.8 93.7 %copy-start.4 = (bf16[2,256,128]{2,1,0:T(8,128)(2,1)S(1)}, bf16[2,256,128]{2,1,0:T(8,128)(2,1)}, u32[]{:S(2)}) copy-start(bf16[2,256,128]{2,1,0:T(8,128)(2,1)} %param.12) | copy-start | bytes 393220
  271.1 100.9 %copy-start.5 = (bf16[128,1024]{1,0:T(8,128)(2,1)S(1)}, bf16[128,1024]{1,0:T(8,128)(2,1)}, u32[]{:S(2)}) copy-start(bf16[128,1024]{1,0:T(8,128)(2,1)} %param.20) | copy-start | bytes 786436
  271.3 100.8 %copy-start.6 = (bf16[128,1024]{1,0:T(8,128)(2,1)S(1)}, bf16[128,1024]{1,0:T(8,128)(2,1)}, u32[]{:S(2)}) copy-start(bf16[128,1024]{1,0:T(8,128)(2,1)} %param.21) | copy-start | bytes 786436
  272.0 209.6 %all-gather.13.cloned.1.call-start = ((), (), s32[]{:S(2)}) async-start(), calls=%async_computation.7 | async-start | bytes 4259840 | tf_op jit(solution)/shard_map/all_gather | solution.py:42
  272.7 294.5 %all-gather.11.cloned.1.call-start = ((), (), s32[]{:S(2)}) async-start(), calls=%async_computation.6 | async-start | bytes 1179648 | tf_op jit(solution)/shard_map/all_gather | solution.py:127
  366.2 4.2 collective-permute-start
  371.1 249.9 %reduce-scatter.3.cloned.1.call-start = ((), (), s32[]{:S(2)}) async-start(), calls=%async_computation.8 | async-start | bytes 1310720 | tf_op jit(solution)/shard_map/reduce_scatter | solution.py:60
  372.1 202.9 %copy-start.2 = (bf16[16,8,8,128]{3,2,1,0:T(8,128)(2,1)}, bf16[16,8,8,128]{3,2,1,0:T(8,128)(2,1)S(1)}, u32[]{:S(2)}) copy-start(bf16[16,8,8,128]{3,2,1,0:T(8,128)(2,1)S(1)} %copy.63) | copy-start | bytes 786436
  567.2 3.6 copy-start.11
  590.8 2.0 copy-start.3
  592.8 3.0 copy-start.12
  598.6 66.3 %reduce-scatter.5.cloned.1.call-start = ((), (), s32[]{:S(2)}) async-start(), calls=%async_computation.9 | async-start | bytes 393216 | tf_op jit(solution)/shard_map/reduce_scatter | solution.py:60
  665.8 5.6 collective-permute-start.1
  (1 other events, 1.2 us)
Sparse Core Ops, SparseCore 0:
  11.2 150.4 all-gather.14
  164.3 100.6 all-gather.6
  272.1 92.2 all-gather.8
  366.5 115.0 all-gather.12
  485.1 82.0 all-gather.10
  598.7 22.2 reduce-scatter.2
  623.8 40.9 reduce-scatter.4
where the time goes:
time: 680 us; the launch traced here: 679 us
  waiting for transfers between devices  556 us (82%)
  matrix products  33.9 us (5%)
  blocking collectives  27.9 us (4%)
  local copies, waits for them, and re-layouts  20.2 us (3%)
  starting transfers between devices  19 us (3%)
  between operations  15.2 us (2%)
    all_gather x2, waiting for transfers between devices, in_one_piece(): lax.all_gather(both, axis, axis=dim, tiled=True)  203 us
    all_gather x1, waiting for transfers between devices, one_gather(): lines, at, gathered = (lax.all_gather(vector, axis), 0, [])  135 us
    all_gather x1, waiting for transfers between devices, on_device(): previous = lax.all_gather(previous_part, TENSOR, axis=1, tiled=True)  85.6 us
    reduce_scatter x2, waiting for transfers between devices, sum_in_order(): blocks = lax.psum_scatter(blocks, axes[k], scatter_dimension=0, tiled=True)  66.2 us
    all_gather x1, waiting for transfers between devices, on_device(): full_mix = lax.all_gather(head_mix, TENSOR, axis=1, tiled=True)  63.7 us
    all_to_all x1, blocking collectives, copy_for_each(): return lax.all_to_all(copies, axis, split_axis=0, concat_axis=0, tiled=True)  27.9 us
    all_to_all x1, starting transfers between devices, copy_for_each(): return lax.all_to_all(copies, axis, split_axis=0, concat_axis=0, tiled=True)  14 us
  transfers between devices with their start and end apart: 10, of which 9 were waited for; matrix products, arithmetic and copies ran while one was open for 3% of the time, Pallas kernels for 0%

commit v1 on v0

v1 whole, which is shorter than its diff:
```python
import math

import jax
import jax.numpy as jnp
from jax import lax
from jax.experimental import pallas as pl
from jax.experimental.pallas import tpu as pltpu
from jax.sharding import PartitionSpec as P

MESH = pl.DeviceIdType.MESH
BF = jnp.bfloat16
F32 = jnp.float32
NT = (((1,), (1,)), ((), ()))
TN = (((0,), (0,)), ((), ()))
NN = (((1,), (0,)), ((), ()))


def dot(a, b, dims=NN):
    return lax.dot_general(a, b, dims, preferred_element_type=F32)


def remote(src, dst, send, recv, device):
    return pltpu.make_async_remote_copy(
        src_ref=src, dst_ref=dst, send_sem=send, recv_sem=recv, device_id=device, device_id_type=MESH
    )


class Ring4:
    def __init__(self, me, device, full, half, send, recv, source=None):
        left, right, far = lax.rem(me + 3, 4), lax.rem(me + 1, 4), lax.rem(me + 2, 4)
        source = full(me) if source is None else source
        self.first = [
            remote(source, full(me), send.at[0], recv.at[0], device(right)),
            remote(source, full(me), send.at[1], recv.at[1], device(left)),
        ]
        self.arrive = [
            remote(full(left), full(left), send.at[0], recv.at[0], device(right)),
            remote(full(right), full(right), send.at[1], recv.at[1], device(left)),
        ]
        self.second = [
            remote(half(left, 0), half(left, 0), send.at[2], recv.at[2], device(right)),
            remote(half(right, 1), half(right, 1), send.at[3], recv.at[3], device(left)),
        ]
        self.last = [
            remote(half(far, 0), half(far, 0), send.at[2], recv.at[2], device(right)),
            remote(half(far, 1), half(far, 1), send.at[3], recv.at[3], device(left)),
        ]

    def start(self):
        for copy in self.first:
            copy.start()

    def middle(self):
        for k in range(2):
            self.arrive[k].wait_recv()
            self.second[k].start()

    def finish(self):
        for copy in self.last:
            copy.wait_recv()

    def drain(self):
        for copy in self.first + self.second:
            copy.wait_send()


def kernel(
    lens, s, n, q, g, wk, wv, wq, wo, wkd, wvd,
    att_out, grad_out,
    we, wqo, wd, sx, nx, qd, gd, mix, prev, gkv, att, part, precv, gsend, grecv,
    lsem, zs, zr, ys, yr, ds, dr, xs, xr, hs, hr, qs, qr, rs, rr, as_, ar,
):
    y, t, e = lax.axis_index("dp"), lax.axis_index("tensor"), lax.axis_index("enc")
    h, x = lax.div(t, 4), lax.rem(t, 4)
    j, c = lax.div(e, 2), lax.rem(e, 2)
    z = h * 8 + j
    before, after = lax.rem(e + 15, 16), lax.rem(e + 1, 16)
    sibling = (y, t, j * 2 + 1 - c)
    partner = (y, (1 - h) * 4 + x, e)

    def along_x(i):
        return (y, h * 4 + i, e)

    def along_y(i):
        return (i, t, e)

    def z_of(k):
        zz = lax.rem(z + k + 16, 16)
        return lax.div(zz, 8), lax.rem(zz, 8)

    def along_z(k):
        hz, jz = z_of(k)
        return (y, hz * 4 + x, jz * 2 + c)

    def lanes(i, width):
        return pl.ds(pl.multiple_of(i * width, width), width)

    blocks = (
        lambda b, yy: we.at[b[0], b[1], c, yy],
        lambda b, yy: wqo.at[b[0], b[1], c, yy],
        lambda b, yy: wd.at[b[0], yy, b[1], c],
    )
    whole = (
        lambda yy, cc: we.at[:, :, cc, yy],
        lambda yy, cc: wqo.at[:, :, cc, yy],
        lambda yy, cc: wd.at[:, yy, :, cc],
    )
    halves = (
        lambda yy, k: we.at[k, :, c, yy],
        lambda yy, k: wqo.at[k, :, c, yy],
        lambda yy, k: wd.at[k, yy, :, c],
    )
    kinds = range(3)
    own = (h, j)

    fetch = []

    def local(src, dst):
        copy = pltpu.make_async_copy(src, dst, lsem.at[len(fetch)])
        copy.start()
        fetch.append(copy)

    local(wk.at[pl.ds(y * 128, 128)], we.at[h, j, c, y, :, 0:128])
    local(wv.at[pl.ds(y * 128, 128)], we.at[h, j, c, y, :, 128:256])
    local(wq.at[pl.ds(y * 16, 16)], wqo.at[h, j, c, y, :, 0:128])
    local(wo.at[pl.ds(y * 16, 16)], wqo.at[h, j, c, y, :, 128:256])
    local(wkd, wd.at[h, y, j, c, :, 0:1024])
    local(wvd, wd.at[h, y, j, c, :, 1024:2048])
    local(s.at[pl.ds(h * 64, 64)], sx.at[t])
    local(n.at[h], nx.at[:, lanes(t, 128)])

    home = [
        pltpu.make_async_copy(q.at[64:128], qd.at[0], lsem.at[8]),
        pltpu.make_async_copy(g.at[64:128], gd.at[0], lsem.at[9]),
    ]

    @pl.when(h == 0)
    def _():
        for copy in home:
            copy.start()

    barrier = pltpu.get_barrier_semaphore()

    def greet(device):
        pl.semaphore_signal(barrier, inc=1, device_id=device, device_id_type=MESH)

    for k in (1, 2, 3):
        greet(along_x(lax.rem(x + k, 4)))
    for k in (1, 3):
        greet(along_y(lax.rem(y + k, 4)))
    for k in (1, -1):
        greet(along_z(k))
    greet(sibling)
    greet(partner)
    greet((y, 4 + x, before))

    @pl.when(h == 1)
    def _():
        greet((y, x, after))
        greet((y, 4 + x, after))

    pl.semaphore_wait(barrier, 10 + 2 * h)

    swaps = [
        remote(s.at[pl.ds((1 - h) * 64, 64)], sx.at[t], hs.at[0], hr.at[0], partner),
        remote(n.at[1 - h], nx.at[:, lanes(t, 128)], hs.at[1], hr.at[1], partner),
    ]
    for copy in swaps:
        copy.start()

    def s_ring(half_of, k, source=None):
        return Ring4(
            x, along_x,
            lambda i: sx.at[half_of * 4 + i],
            lambda i, m: sx.at[half_of * 4 + i, m * 32 : m * 32 + 32],
            xs.at[k], xr.at[k], source,
        )

    def wide_ring(ref, half_of, k, source=None):
        return Ring4(
            x, along_x,
            lambda i: ref.at[:, lanes(half_of * 4 + i, 128)],
            lambda i, m: ref.at[m * 128 : m * 128 + 128, lanes(half_of * 4 + i, 128)],
            xs.at[k], xr.at[k], source,
        )

    s_own = s_ring(h, 0, s.at[pl.ds(h * 64, 64)])
    n_own = wide_ring(nx, h, 1, n.at[h])
    s_other = s_ring(1 - h, 2)
    n_other = wide_ring(nx, 1 - h, 3)
    s_own.start()
    n_own.start()

    for copy in fetch[:6]:
        copy.wait()

    def y_send(b):
        out = []
        for k in kinds:
            for d, to in ((0, 1), (1, 3)):
                ref = blocks[k](b, y)
                out.append(remote(ref, ref, ys.at[k, d], yr.at[k, d], along_y(lax.rem(y + to, 4))))
        for copy in out:
            copy.start()

    def z_copy(k, d, step, b):
        ref = blocks[k](b, y)
        return remote(ref, ref, zs.at[k, d, step], zr.at[k, d, step], along_z(1 - 2 * d))

    lasts = (8, 7)
    sent = []
    for d in (0, 1):
        for k in kinds:
            copy = z_copy(k, d, 0, own)
            copy.start()
            sent.append(copy)
    y_send(own)

    to_far = [
        remote(q.at[0:64], qd.at[h], qs.at[0], qr.at[0, h], (y, 4 + x, before)),
        remote(g.at[0:64], gd.at[h], qs.at[1], qr.at[1, h], (y, 4 + x, before)),
    ]
    to_near = [
        remote(q.at[64:128], qd.at[1], qs.at[2], qr.at[0, 1], partner),
        remote(g.at[64:128], gd.at[1], qs.at[3], qr.at[1, 1], partner),
    ]

    for step in range(1, 9):
        for d in (0, 1):
            if step > lasts[d]:
                continue
            b = z_of(-step if d == 0 else step)
            for k in kinds:
                z_copy(k, d, step - 1, b).wait_recv()
                if step < lasts[d]:
                    copy = z_copy(k, d, step, b)
                    copy.start()
                    sent.append(copy)
            y_send(b)
        if step == 2:
            s_own.middle()
            n_own.middle()
        if step == 4:
            for copy in to_far:
                copy.start()

            @pl.when(h == 1)
            def _():
                for copy in to_near:
                    copy.start()

        if step == 5:
            for copy in swaps:
                copy.wait_recv()
            s_other.start()
            n_other.start()
        if step == 7:
            s_other.middle()
            n_other.middle()

    left, right, far = lax.rem(y + 3, 4), lax.rem(y + 1, 4), lax.rem(y + 2, 4)

    def d_copy(k, i, yy, cc):
        ref = whole[k](yy, cc)
        return remote(ref, ref, ds.at[k, i], dr.at[k, i], sibling)

    for k in kinds:
        d_copy(k, 0, y, c).start()
    for k in kinds:
        for d, yy in ((0, left), (1, right)):
            ref = whole[k](yy, c)
            remote(ref, ref, ys.at[k, d], yr.at[k, d], along_y(right)).wait_recv()
            to = halves[k](yy, d)
            remote(to, to, ys.at[k, 2 + d], yr.at[k, 2 + d], along_y(right if d == 0 else left)).start()
            d_copy(k, 1 + d, yy, c).start()

    def y_finish(k):
        for d in (0, 1):
            to = halves[k](far, d)
            remote(to, to, ys.at[k, 2 + d], yr.at[k, 2 + d], along_y(right)).wait_recv()
        d_copy(k, 3, far, c).start()

    def d_finish(k):
        for i, yy in enumerate((y, left, right, far)):
            d_copy(k, i, yy, 1 - c).wait_recv()

    y_finish(0)
    y_finish(1)
    for copy in fetch[6:]:
        copy.wait()
    for ring in (s_own, n_own, s_other, n_other):
        ring.finish()
    d_finish(0)
    d_finish(1)

    first = lax.broadcasted_iota(jnp.int32, (64, 128), 1) < 64
    mix_rings = []
    for hh in (0, 1):
        total = jnp.zeros((64, 256), F32)
        for tt in range(8):
            total = total + dot(sx[tt], we[hh, tt].reshape(1024, 256))
        both = total.astype(BF)
        key, value = both[:, :128], both[:, 128:]
        query = dot(nx[...], wqo[hh, :, :, :, :, 0:128].reshape(1024, 128)).astype(BF)
        mixed = jnp.zeros((256, 128), F32)
        zero = jnp.zeros((64, 128), BF)
        for keep in (first, jnp.logical_not(first)):
            score = dot(query, jnp.where(keep, key, zero), NT) * (1.0 / math.sqrt(64))
            score = jnp.exp(score - jnp.max(score, axis=-1, keepdims=True))
            weight = (score / jnp.sum(score, axis=-1, keepdims=True)).astype(BF)
            mixed = mixed + dot(weight, jnp.where(keep, value, zero))
        mix[:, lanes(hh * 4 + x, 128)] = mixed.astype(BF)
        ring = wide_ring(mix, hh, 4 + hh)
        ring.start()
        mix_rings.append(ring)
    for ring in mix_rings:
        ring.middle()
    for ring in mix_rings:
        ring.finish()
    prev_rings = []
    for hh in (0, 1):
        at = lanes(hh * 4 + x, 128)
        out = dot(mix[...], wqo[hh, :, :, :, :, 128:256].reshape(1024, 128))
        prev[:, at] = (nx[:, at].astype(F32) + out).astype(BF)
        ring = wide_ring(prev, hh, 6 + hh)
        ring.start()
        prev_rings.append(ring)
    y_finish(2)
    for ring in prev_rings:
        ring.middle()
    for ring in prev_rings:
        ring.finish()
    d_finish(2)

    def q_wait(slot):
        remote(q.at[0:64], qd.at[slot], qs.at[0], qr.at[0, slot], partner).wait_recv()
        remote(g.at[0:64], gd.at[slot], qs.at[1], qr.at[1, slot], partner).wait_recv()

    @pl.when(h == 0)
    def _():
        for copy in home:
            copy.wait()

    @pl.when(h == 1)
    def _():
        q_wait(0)

    q_wait(1)

    token = lax.rem(e * 2 + h + 1, 32) * 64
    position = token + lax.broadcasted_iota(jnp.int32, (64, 128), 0)
    live = jnp.logical_and(position < lens[0], position >= 64)
    scale = 1.0 / math.sqrt(128)

    def heads(turn, carry):
        hh, base = lax.div(turn, 2), lax.rem(turn, 2) * 512
        source = prev[...]
        at_key = pl.ds(pl.multiple_of(base, 512), 512)
        at_value = pl.ds(pl.multiple_of(1024 + base, 512), 512)
        keys = dot(source, wd[hh, :, :, :, :, at_key].reshape(1024, 512)).astype(BF)
        values = dot(source, wd[hh, :, :, :, :, at_value].reshape(1024, 512)).astype(BF)
        for a in range(4):
            at = pl.ds(pl.multiple_of(base + a * 128, 128), 128)
            later = pl.ds(pl.multiple_of(1024 + base + a * 128, 128), 128)
            key, value = keys[:, a * 128 : a * 128 + 128], values[:, a * 128 : a * 128 + 128]
            query = qd[hh, :, at]
            score = dot(query, key, NT) * scale
            score = jnp.exp(score - jnp.max(score, axis=-1, keepdims=True))
            probs = score / jnp.sum(score, axis=-1, keepdims=True)
            low = probs.astype(BF)
            att[hh, :, at] = jnp.where(live, dot(low, value), 0.0).astype(BF)
            cot = jnp.where(live, gd[hh, :, at].astype(F32), 0.0).astype(BF)
            gkv[hh, :, later] = dot(low, cot, TN).astype(BF)
            slope = dot(cot, value, NT)
            inner = jnp.sum(slope * probs, axis=-1, keepdims=True)
            slope = (probs * (slope - inner) * scale).astype(BF)
            gkv[hh, :, at] = dot(slope, query, TN).astype(BF)
        return carry

    lax.fori_loop(0, 4, heads, 0)

    low_rows, high_rows = pl.ds(0, 64), pl.ds(64, 64)
    near = remote(att.at[1], att_out.at[high_rows], as_.at[1], ar.at[1], partner)
    onward = [
        remote(att.at[k], att_out.at[low_rows], as_.at[k], ar.at[0], (y, k * 4 + x, after))
        for k in (0, 1)
    ]

    @pl.when(h == 0)
    def _():
        near.start()
        att_out[64:128, :] = att[0]

    @pl.when(h == 1)
    def _():
        for copy in onward:
            copy.start()

    def share(to):
        total = jnp.zeros((256, 256), F32)
        for hh in (0, 1):
            rows = [
                wd[hh, lax.div(k * 4 + to, 2), pl.ds(lax.rem(to, 2) * 4, 4)].reshape(128, 2048)
                for k in (0, 1)
            ]
            total = total + dot(gkv[hh], jnp.concatenate(rows, axis=0), NT)
        return total

    shares = []
    for k in (2, 1, 3):
        to = lax.rem(x + k, 4)
        part[k - 1] = share(to).astype(BF)
        copy = remote(part.at[k - 1], precv.at[k - 1], rs.at[k - 1], rr.at[k - 1], along_x(to))
        copy.start()
        shares.append(copy)
    total = share(x)
    for k in (1, 3, 2):
        remote(part.at[k - 1], precv.at[k - 1], rs.at[k - 1], rr.at[k - 1], partner).wait_recv()
        total = total + precv[k - 1].astype(F32)
    mine = jnp.where(h == 0, total[:, :128], total[:, 128:])
    other = jnp.where(h == 0, total[:, 128:], total[:, :128])
    gsend[...] = other.astype(BF)
    give = remote(gsend, grecv, hs.at[2], hr.at[2], partner)
    give.start()
    grad_out[h] = mine

    for copy in sent + swaps + to_far + shares:
        copy.wait_send()
    for ring in [s_own, n_own, s_other, n_other] + mix_rings + prev_rings:
        ring.drain()
    for k in kinds:
        for d in (0, 1):
            ref = whole[k](y, c)
            remote(ref, ref, ys.at[k, d], yr.at[k, d], along_y(right)).wait_send()
            to = halves[k](far, d)
            remote(to, to, ys.at[k, 2 + d], yr.at[k, 2 + d], along_y(right)).wait_send()
        for i in range(4):
            d_copy(k, i, y, c).wait_send()

    @pl.when(h == 0)
    def _():
        near.wait_send()

    @pl.when(h == 1)
    def _():
        for copy in to_near + onward:
            copy.wait_send()
        remote(att.at[0], att_out.at[high_rows], as_.at[1], ar.at[1], partner).wait_recv()

    remote(att.at[0], att_out.at[low_rows], as_.at[0], ar.at[0], partner).wait_recv()
    give.wait()
    grad_out[1 - h] = grecv[...].astype(F32)


def on_device(span_states, neighbours, lengths, wq, wk, wv, wo, wkd, wvd, queries, grad_out):
    dma = pltpu.SemaphoreType.DMA
    hbm = pl.BlockSpec(memory_space=pltpu.HBM)
    vmem = pl.BlockSpec(memory_space=pltpu.VMEM)
    return pl.pallas_call(
        kernel,
        out_shape=(
            jax.ShapeDtypeStruct((128, 1024), BF),
            jax.ShapeDtypeStruct((2, 256, 128), F32),
        ),
        in_specs=[pl.BlockSpec(memory_space=pltpu.SMEM)] + [hbm] * 10,
        out_specs=(vmem, vmem),
        scratch_shapes=[
            pltpu.VMEM((2, 8, 2, 4, 128, 256), BF),
            pltpu.VMEM((2, 8, 2, 4, 16, 256), BF),
            pltpu.VMEM((2, 4, 8, 2, 16, 2048), BF),
            pltpu.VMEM((8, 64, 1024), BF),
            pltpu.VMEM((256, 1024), BF),
            pltpu.VMEM((2, 64, 1024), BF),
            pltpu.VMEM((2, 64, 1024), BF),
            pltpu.VMEM((256, 1024), BF),
            pltpu.VMEM((256, 1024), BF),
            pltpu.VMEM((2, 256, 2048), BF),
            pltpu.VMEM((2, 64, 1024), BF),
            pltpu.VMEM((3, 256, 256), BF),
            pltpu.VMEM((3, 256, 256), BF),
            pltpu.VMEM((256, 128), BF),
            pltpu.VMEM((256, 128), BF),
            dma((10,)),
            dma((3, 2, 8)),
            dma((3, 2, 8)),
            dma((3, 4)),
            dma((3, 4)),
            dma((3, 4)),
            dma((3, 4)),
            dma((8, 4)),
            dma((8, 4)),
            dma((3,)),
            dma((3,)),
            dma((4,)),
            dma((2, 2)),
            dma((3,)),
            dma((3,)),
            dma((2,)),
            dma((2,)),
        ],
        compiler_params=pltpu.CompilerParams(
            collective_id=0, has_side_effects=True, vmem_limit_bytes=58 * 1024 * 1024
        ),
    )(lengths, span_states, neighbours, queries, grad_out, wk, wv, wq, wo, wkd, wvd)


def solution(mesh):
    rows = P(("dp", "enc"), "tensor")
    spans = P(("dp", "enc"), None, "tensor")
    weight = P("enc", "tensor")
    return jax.shard_map(
        on_device,
        mesh=mesh,
        in_specs=(rows, spans, P("dp"), weight, weight, weight, weight, rows, rows, rows, rows),
        out_specs=(rows, spans),
        check_vma=False,
    )
```

time: 680 us -> 175 us (0.26)
  waiting for transfers between devices: 556 us -> 0 us
  Pallas kernels: 0 us -> 169 us
  matrix products: 33.9 us -> 0 us
  blocking collectives: 27.9 us -> 0 us
  starting transfers between devices: 19 us -> 0 us
  local copies, waits for them, and re-layouts: 20.2 us -> 2.42 us
  between operations: 15.2 us -> 1.3 us
    all_gather x5 -> x0, waiting for transfers between devices: 487 us -> none  [the longest x2 203 us: in_one_piece(): lax.all_gather(both, axis, axis=dim, tiled=True)]
    pallas_call x0 -> x1, Pallas kernels: none -> 169 us  [on_device(): pl.pallas_call(kernel, out_shape=(jax.ShapeDtypeStruct((128, 1024), BF),...]
    reduce_scatter x2 -> x0, waiting for transfers between devices: 66.2 us -> none  [sum_in_order(): blocks = lax.psum_scatter(blocks, axes[k], scatter_dimension=0, tiled=True)]
    dot_general x15 -> x0, matrix products: 33.9 us -> none  [the longest x1 8.72 us: on_device(): jnp.einsum('chmk,cmhd->ckhd', grad_scores, query_dec, preferred_element_t...]
    all_to_all x1 -> x0, blocking collectives: 27.9 us -> none  [copy_for_each(): return lax.all_to_all(copies, axis, split_axis=0, concat_axis=0, tiled=True)]
    all_to_all x1 -> x0, starting transfers between devices: 14 us -> none  [copy_for_each(): return lax.all_to_all(copies, axis, split_axis=0, concat_axis=0, tiled=True)]
  transfers between devices with their start and end apart: 10 -> 0, of which waited for: 9 -> 0; matrix products, arithmetic and copies ran while one was open for 3% -> 0% of each run, Pallas kernels for 0% -> 0%
where the time goes in v1:
time: 175 us; the launch traced here: 173 us
  Pallas kernels  169 us (97%)
  local copies, waits for them, and re-layouts  2.42 us (1%)
    pallas_call x1, Pallas kernels, on_device(): pl.pallas_call(kernel, out_shape=(jax.ShapeDtypeStruct((128, 1024), BF),...  169 us

profile of v1, /device:TPU:1, one launch (start us, length us, event | category | flops | bytes accessed | tf_op | source)
XLA Modules:
  0.0 173.1 jit_solution(15846115820208940485)
XLA Ops:
  1.3 169.4 %shard_map.122 = (bf16[128,1024]{1,0:T(8,128)(2,1)}, f32[2,256,128]{2,1,0:T(8,128)}) custom-call(s32[1]{0:T(128)S(6)} %copy.15.lens, bf16[128,1024]{1,0:T(8,128)(2,1)} %s.1, bf16[2,256,128]{2,1,0:T(8,128)(2,1)} %n.1, bf16[128,1024]{1,0:T(8,128)(2,1)} %q.1, bf16[128,1024]{1,0:T(8,128)(2,1)} %g.1, bf16[512,128]{1,0:T(8,128)(2,1)} %wk.1, bf16[512,128]{1,0:T(8,128)(2,1)} %wv.1, ...), custom_call_target="tpu_custom_call" | custom-call | tf_op jit(solution)/shard_map/pallas_call | solution.py:459
  170.7 0.0 copy-start
  170.7 1.7 copy.16
  172.4 0.0 copy-done
  172.4 0.7 copy.17
Async XLA Ops:
  170.7 1.7 copy-start

commit v2 on v1

--- a/solution.py
+++ b/solution.py
@@ -67,16 +67,19 @@
 def kernel(
     lens, s, n, q, g, wk, wv, wq, wo, wkd, wvd,
     att_out, grad_out,
-    we, wqo, wd, sx, nx, qd, gd, mix, prev, gkv, att, part, precv, gsend, grecv,
+    we, wqo, wd, sx, nx, qd, gd, kvp, kvs, kvr, mix, prev, gkv, att, part, precv, gsend, grecv,
+    n_pass, kv_pass, qg_pass, att_pass, g_pass,
     lsem, zs, zr, ys, yr, ds, dr, xs, xr, hs, hr, qs, qr, rs, rr, as_, ar,
 ):
     y, t, e = lax.axis_index("dp"), lax.axis_index("tensor"), lax.axis_index("enc")
     h, x = lax.div(t, 4), lax.rem(t, 4)
     j, c = lax.div(e, 2), lax.rem(e, 2)
     z = h * 8 + j
+    way = 1 - 2 * c
     before, after = lax.rem(e + 15, 16), lax.rem(e + 1, 16)
     sibling = (y, t, j * 2 + 1 - c)
-    partner = (y, (1 - h) * 4 + x, e)
+    near_rows = pl.ds(pl.multiple_of(h * 64, 64), 64)
+    far_rows = pl.ds(pl.multiple_of((1 - h) * 64, 64), 64)
 
     def along_x(i):
         return (y, h * 4 + i, e)
@@ -88,25 +91,31 @@
         zz = lax.rem(z + k + 16, 16)
         return lax.div(zz, 8), lax.rem(zz, 8)
 
-    def along_z(k):
+    def along_z(k, core=c):
         hz, jz = z_of(k)
-        return (y, hz * 4 + x, jz * 2 + c)
+        return (y, hz * 4 + x, jz * 2 + core)
 
     def lanes(i, width):
         return pl.ds(pl.multiple_of(i * width, width), width)
 
+    next_chip = along_z(way)
+    onto = along_z(8 - way)
+    from_h, from_j = z_of(-way)
+    from_e = from_j * 2 + c
+
+    use = pl.ds(h * 4, 4)
     blocks = (
         lambda b, yy: we.at[b[0], b[1], c, yy],
         lambda b, yy: wqo.at[b[0], b[1], c, yy],
         lambda b, yy: wd.at[b[0], yy, b[1], c],
     )
     whole = (
-        lambda yy, cc: we.at[:, :, cc, yy],
+        lambda yy, cc: we.at[:, use, cc, yy],
         lambda yy, cc: wqo.at[:, :, cc, yy],
         lambda yy, cc: wd.at[:, yy, :, cc],
     )
     halves = (
-        lambda yy, k: we.at[k, :, c, yy],
+        lambda yy, k: we.at[k, use, c, yy],
         lambda yy, k: wqo.at[k, :, c, yy],
         lambda yy, k: wd.at[k, yy, :, c],
     )
@@ -126,7 +135,7 @@
     local(wo.at[pl.ds(y * 16, 16)], wqo.at[h, j, c, y, :, 128:256])
     local(wkd, wd.at[h, y, j, c, :, 0:1024])
     local(wvd, wd.at[h, y, j, c, :, 1024:2048])
-    local(s.at[pl.ds(h * 64, 64)], sx.at[t])
+    local(s, sx.at[x])
     local(n.at[h], nx.at[:, lanes(t, 128)])
 
     home = [
@@ -144,37 +153,33 @@
     def greet(device):
         pl.semaphore_signal(barrier, inc=1, device_id=device, device_id_type=MESH)
 
-    for k in (1, 2, 3):
+    for k in (7, -7):
+        greet(along_z(k))
+        greet(along_z(k, 1 - c))
+    greet((y, 4 + x, before))
+
+    @pl.when(h == 1)
+    def _():
+        greet((y, x, after))
+        greet((y, 4 + x, after))
+
+    for k in (2, 1, 3):
         greet(along_x(lax.rem(x + k, 4)))
     for k in (1, 3):
         greet(along_y(lax.rem(y + k, 4)))
     for k in (1, -1):
         greet(along_z(k))
     greet(sibling)
-    greet(partner)
-    greet((y, 4 + x, before))
-
-    @pl.when(h == 1)
-    def _():
-        greet((y, x, after))
-        greet((y, 4 + x, after))
-
-    pl.semaphore_wait(barrier, 10 + 2 * h)
-
-    swaps = [
-        remote(s.at[pl.ds((1 - h) * 64, 64)], sx.at[t], hs.at[0], hr.at[0], partner),
-        remote(n.at[1 - h], nx.at[:, lanes(t, 128)], hs.at[1], hr.at[1], partner),
-    ]
-    for copy in swaps:
-        copy.start()
-
-    def s_ring(half_of, k, source=None):
-        return Ring4(
-            x, along_x,
-            lambda i: sx.at[half_of * 4 + i],
-            lambda i, m: sx.at[half_of * 4 + i, m * 32 : m * 32 + 32],
-            xs.at[k], xr.at[k], source,
+    pl.semaphore_wait(barrier, 13 + 2 * h)
+
+    def pass_on(k, src, room, dst):
+        return (
+            remote(src, room, hs.at[0, k], hr.at[0, k], next_chip),
+            remote(room, dst, hs.at[1, k], hr.at[1, k], onto),
         )
+
+    n_swap = pass_on(0, n.at[1 - h], n_pass, nx.at[:, lanes(from_h * 4 + x, 128)])
+    n_swap[0].start()
 
     def wide_ring(ref, half_of, k, source=None):
         return Ring4(
@@ -184,24 +189,29 @@
             xs.at[k], xr.at[k], source,
         )
 
-    s_own = s_ring(h, 0, s.at[pl.ds(h * 64, 64)])
+    s_ring = Ring4(
+        x, along_x, lambda i: sx.at[i], lambda i, m: sx.at[i, m * 64 : m * 64 + 64], xs.at[0], xr.at[0], s
+    )
     n_own = wide_ring(nx, h, 1, n.at[h])
-    s_other = s_ring(1 - h, 2)
-    n_other = wide_ring(nx, 1 - h, 3)
-    s_own.start()
+    n_other = wide_ring(nx, 1 - h, 2)
     n_own.start()
+    s_ring.start()
 
     for copy in fetch[:6]:
         copy.wait()
 
     def y_send(b):
-        out = []
-        for k in kinds:
+        def to_both(k):
             for d, to in ((0, 1), (1, 3)):
                 ref = blocks[k](b, y)
-                out.append(remote(ref, ref, ys.at[k, d], yr.at[k, d], along_y(lax.rem(y + to, 4))))
-        for copy in out:
-            copy.start()
+                remote(ref, ref, ys.at[k, d], yr.at[k, d], along_y(lax.rem(y + to, 4))).start()
+
+        @pl.when(lax.div(b[1], 4) == h)
+        def _():
+            to_both(0)
+
+        to_both(1)
+        to_both(2)
 
     def z_copy(k, d, step, b):
         ref = blocks[k](b, y)
@@ -215,15 +225,6 @@
             copy.start()
             sent.append(copy)
     y_send(own)
-
-    to_far = [
-        remote(q.at[0:64], qd.at[h], qs.at[0], qr.at[0, h], (y, 4 + x, before)),
-        remote(g.at[0:64], gd.at[h], qs.at[1], qr.at[1, h], (y, 4 + x, before)),
-    ]
-    to_near = [
-        remote(q.at[64:128], qd.at[1], qs.at[2], qr.at[0, 1], partner),
-        remote(g.at[64:128], gd.at[1], qs.at[3], qr.at[1, 1], partner),
-    ]
 
     for step in range(1, 9):
         for d in (0, 1):
@@ -237,26 +238,15 @@
                     copy.start()
                     sent.append(copy)
             y_send(b)
-        if step == 2:
-            s_own.middle()
+        if step == 1:
+            n_swap[0].wait_recv()
+            n_swap[1].start()
             n_own.middle()
-        if step == 4:
-            for copy in to_far:
-                copy.start()
-
-            @pl.when(h == 1)
-            def _():
-                for copy in to_near:
-                    copy.start()
-
-        if step == 5:
-            for copy in swaps:
-                copy.wait_recv()
-            s_other.start()
+        if step == 3:
+            s_ring.middle()
+        if step == 6:
+            n_swap[1].wait_recv()
             n_other.start()
-        if step == 7:
-            s_other.middle()
-            n_other.middle()
 
     left, right, far = lax.rem(y + 3, 4), lax.rem(y + 1, 4), lax.rem(y + 2, 4)
 
@@ -264,9 +254,7 @@
         ref = whole[k](yy, cc)
         return remote(ref, ref, ds.at[k, i], dr.at[k, i], sibling)
 
-    for k in kinds:
-        d_copy(k, 0, y, c).start()
-    for k in kinds:
+    def y_middle(k):
         for d, yy in ((0, left), (1, right)):
             ref = whole[k](yy, c)
             remote(ref, ref, ys.at[k, d], yr.at[k, d], along_y(right)).wait_recv()
@@ -284,37 +272,89 @@
         for i, yy in enumerate((y, left, right, far)):
             d_copy(k, i, yy, 1 - c).wait_recv()
 
+    for k in kinds:
+        d_copy(k, 0, y, c).start()
+    for k in kinds:
+        y_middle(k)
+
+    q_to, q_from = [], []
+    for k, (ref, there) in enumerate(((q, qd), (g, gd))):
+        q_to.append((
+            remote(ref.at[near_rows], qg_pass.at[k], qs.at[0, k], qr.at[0, k], next_chip),
+            remote(ref.at[0:64], there.at[h], qs.at[1, k], qr.at[1 + h, k], (y, 4 + x, before)),
+        ))
+        q_from.append(
+            remote(
+                qg_pass.at[k], there.at[from_h], qs.at[2, k], qr.at[1 + from_h, k],
+                (y, (1 - from_h) * 4 + x, lax.rem(from_e + 15 + from_h, 16)),
+            )
+        )
+    sends_far = jnp.logical_or(h == 1, c == 1)
+    sends_direct = jnp.logical_or(h == 1, c == 0)
+    passes_q = jnp.logical_or(from_h == 1, c == 1)
+
     y_finish(0)
     y_finish(1)
+    n_other.middle()
     for copy in fetch[6:]:
         copy.wait()
-    for ring in (s_own, n_own, s_other, n_other):
+    for ring in (s_ring, n_own):
         ring.finish()
     d_finish(0)
+
+    for hh in (0, 1):
+        total = jnp.zeros((128, 256), F32)
+        for i in range(4):
+            total = total + dot(sx[i], we[hh, h * 4 + i].reshape(1024, 256))
+        kvp[hh] = total
+        kvs[hh] = kvp[hh, far_rows].astype(BF)
+    kv_swap = pass_on(1, kvs, kv_pass, kvr)
+    kv_swap[0].start()
+    n_other.finish()
     d_finish(1)
-
+    kv_swap[0].wait_recv()
+    kv_swap[1].start()
+
+    @pl.when(sends_far)
+    def _():
+        for pair in q_to:
+            pair[0].start()
+
+    @pl.when(sends_direct)
+    def _():
+        for pair in q_to:
+            pair[1].start()
+
+    queries = []
+    for hh in (0, 1):
+        queries.append(dot(nx[...], wqo[hh, :, :, :, :, 0:128].reshape(1024, 128)).astype(BF))
+
+    @pl.when(passes_q)
+    def _():
+        for k in (0, 1):
+            q_to[k][0].wait_recv()
+            q_from[k].start()
+
+    kv_swap[1].wait_recv()
     first = lax.broadcasted_iota(jnp.int32, (64, 128), 1) < 64
     mix_rings = []
     for hh in (0, 1):
-        total = jnp.zeros((64, 256), F32)
-        for tt in range(8):
-            total = total + dot(sx[tt], we[hh, tt].reshape(1024, 256))
-        both = total.astype(BF)
+        both = (kvp[hh, near_rows] + kvr[hh].astype(F32)).astype(BF)
         key, value = both[:, :128], both[:, 128:]
-        query = dot(nx[...], wqo[hh, :, :, :, :, 0:128].reshape(1024, 128)).astype(BF)
         mixed = jnp.zeros((256, 128), F32)
         zero = jnp.zeros((64, 128), BF)
         for keep in (first, jnp.logical_not(first)):
-            score = dot(query, jnp.where(keep, key, zero), NT) * (1.0 / math.sqrt(64))
+            score = dot(queries[hh], jnp.where(keep, key, zero), NT) * (1.0 / math.sqrt(64))
             score = jnp.exp(score - jnp.max(score, axis=-1, keepdims=True))
             weight = (score / jnp.sum(score, axis=-1, keepdims=True)).astype(BF)
             mixed = mixed + dot(weight, jnp.where(keep, value, zero))
         mix[:, lanes(hh * 4 + x, 128)] = mixed.astype(BF)
-        ring = wide_ring(mix, hh, 4 + hh)
+        ring = wide_ring(mix, hh, 3 + hh)
         ring.start()
         mix_rings.append(ring)
     for ring in mix_rings:
         ring.middle()
+    y_finish(2)
     for ring in mix_rings:
         ring.finish()
     prev_rings = []
@@ -322,10 +362,9 @@
         at = lanes(hh * 4 + x, 128)
         out = dot(mix[...], wqo[hh, :, :, :, :, 128:256].reshape(1024, 128))
         prev[:, at] = (nx[:, at].astype(F32) + out).astype(BF)
-        ring = wide_ring(prev, hh, 6 + hh)
+        ring = wide_ring(prev, hh, 5 + hh)
         ring.start()
         prev_rings.append(ring)
-    y_finish(2)
     for ring in prev_rings:
         ring.middle()
     for ring in prev_rings:
@@ -333,8 +372,8 @@
     d_finish(2)
 
     def q_wait(slot):
-        remote(q.at[0:64], qd.at[slot], qs.at[0], qr.at[0, slot], partner).wait_recv()
-        remote(g.at[0:64], gd.at[slot], qs.at[1], qr.at[1, slot], partner).wait_recv()
+        for k, (ref, there) in enumerate(((q, qd), (g, gd))):
+            remote(ref.at[0:64], there.at[slot], qs.at[1, k], qr.at[1 + slot, k], next_chip).wait_recv()
 
     @pl.when(h == 0)
     def _():
@@ -353,7 +392,7 @@
     scale = 1.0 / math.sqrt(128)
 
     def heads(turn, carry):
-        hh, base = lax.div(turn, 2), lax.rem(turn, 2) * 512
+        hh, base = lax.rem(1 - h + lax.div(turn, 2), 2), lax.rem(turn, 2) * 512
         source = prev[...]
         at_key = pl.ds(pl.multiple_of(base, 512), 512)
         at_value = pl.ds(pl.multiple_of(1024 + base, 512), 512)
@@ -377,56 +416,83 @@
             gkv[hh, :, at] = dot(slope, query, TN).astype(BF)
         return carry
 
-    lax.fori_loop(0, 4, heads, 0)
-
-    low_rows, high_rows = pl.ds(0, 64), pl.ds(64, 64)
-    near = remote(att.at[1], att_out.at[high_rows], as_.at[1], ar.at[1], partner)
-    onward = [
-        remote(att.at[k], att_out.at[low_rows], as_.at[k], ar.at[0], (y, k * 4 + x, after))
-        for k in (0, 1)
-    ]
+    lax.fori_loop(0, 2, heads, 0)
+
+    low_rows = pl.ds(0, 64)
+    att_far = remote(att.at[1 - h], att_pass, as_.at[0], ar.at[2], next_chip)
+    att_direct = remote(att.at[0], att_out.at[low_rows], as_.at[0], ar.at[0], (y, x, after))
+    att_near = remote(att.at[1], att_out.at[low_rows], as_.at[1], ar.at[0], (y, 4 + x, after))
+    att_on = remote(
+        att_pass, att_out.at[pl.ds(pl.multiple_of((1 - from_h) * 64, 64), 64)], as_.at[2], ar.at[1 - from_h],
+        (y, (1 - from_h) * 4 + x, lax.rem(from_e + from_h, 16)),
+    )
+    direct = jnp.logical_and(h == 1, c == 1)
+    passes_att = jnp.logical_or(from_h == 0, c == 0)
+
+    @pl.when(direct)
+    def _():
+        att_direct.start()
+
+    @pl.when(jnp.logical_not(direct))
+    def _():
+        att_far.start()
+
+    lax.fori_loop(2, 4, heads, 0)
+
+    @pl.when(passes_att)
+    def _():
+        att_far.wait_recv()
+        att_on.start()
 
     @pl.when(h == 0)
     def _():
-        near.start()
         att_out[64:128, :] = att[0]
 
     @pl.when(h == 1)
     def _():
-        for copy in onward:
+        att_near.start()
+
+    def share(k, to):
+        total = jnp.zeros((256, 128), F32)
+        for hh in (0, 1):
+            rows = wd[hh, lax.div(k * 4 + to, 2), pl.ds(lax.rem(to, 2) * 4, 4)].reshape(128, 2048)
+            total = total + dot(gkv[hh], rows, NT)
+        return total
+
+    shares = []
+
+    def give_shares(i, k):
+        for m in (2, 1, 3):
+            to = lax.rem(x + m, 4)
+            part[i, m - 1] = share(k, to).astype(BF)
+            copy = remote(part.at[i, m - 1], precv.at[i, m - 1], rs.at[i, m - 1], rr.at[i, m - 1], along_x(to))
             copy.start()
-
-    def share(to):
-        total = jnp.zeros((256, 256), F32)
-        for hh in (0, 1):
-            rows = [
-                wd[hh, lax.div(k * 4 + to, 2), pl.ds(lax.rem(to, 2) * 4, 4)].reshape(128, 2048)
-                for k in (0, 1)
-            ]
-            total = total + dot(gkv[hh], jnp.concatenate(rows, axis=0), NT)
+            shares.append(copy)
+
+    def take_shares(i, total):
+        for m in (1, 3, 2):
+            remote(
+                part.at[i, m - 1], precv.at[i, m - 1], rs.at[i, m - 1], rr.at[i, m - 1], next_chip
+            ).wait_recv()
+            total = total + precv[i, m - 1].astype(F32)
         return total
 
-    shares = []
-    for k in (2, 1, 3):
-        to = lax.rem(x + k, 4)
-        part[k - 1] = share(to).astype(BF)
-        copy = remote(part.at[k - 1], precv.at[k - 1], rs.at[k - 1], rr.at[k - 1], along_x(to))
-        copy.start()
-        shares.append(copy)
-    total = share(x)
-    for k in (1, 3, 2):
-        remote(part.at[k - 1], precv.at[k - 1], rs.at[k - 1], rr.at[k - 1], partner).wait_recv()
-        total = total + precv[k - 1].astype(F32)
-    mine = jnp.where(h == 0, total[:, :128], total[:, 128:])
-    other = jnp.where(h == 0, total[:, 128:], total[:, :128])
-    gsend[...] = other.astype(BF)
-    give = remote(gsend, grecv, hs.at[2], hr.at[2], partner)
-    give.start()
-    grad_out[h] = mine
-
-    for copy in sent + swaps + to_far + shares:
+    give_shares(0, 1 - h)
+    total = share(1 - h, x)
+    gsend[...] = take_shares(0, total).astype(BF)
+    g_swap = pass_on(2, gsend, g_pass, grecv)
+    g_swap[0].start()
+    give_shares(1, h)
+    g_swap[0].wait_recv()
+    g_swap[1].start()
+    grad_out[h] = take_shares(1, share(h, x))
+
+    for copy in sent + shares:
         copy.wait_send()
-    for ring in [s_own, n_own, s_other, n_other] + mix_rings + prev_rings:
+    for pair in (n_swap, kv_swap, g_swap):
+        for copy in pair:
+            copy.wait_send()
+    for ring in [s_ring, n_own, n_other] + mix_rings + prev_rings:
         ring.drain()
     for k in kinds:
         for d in (0, 1):
@@ -437,18 +503,40 @@
         for i in range(4):
             d_copy(k, i, y, c).wait_send()
 
-    @pl.when(h == 0)
-    def _():
-        near.wait_send()
+    @pl.when(sends_far)
+    def _():
+        for pair in q_to:
+            pair[0].wait_send()
+
+    @pl.when(sends_direct)
+    def _():
+        for pair in q_to:
+            pair[1].wait_send()
+
+    @pl.when(passes_q)
+    def _():
+        for copy in q_from:
+            copy.wait_send()
+
+    @pl.when(direct)
+    def _():
+        att_direct.wait_send()
+
+    @pl.when(jnp.logical_not(direct))
+    def _():
+        att_far.wait_send()
+
+    @pl.when(passes_att)
+    def _():
+        att_on.wait_send()
 
     @pl.when(h == 1)
     def _():
-        for copy in to_near + onward:
-            copy.wait_send()
-        remote(att.at[0], att_out.at[high_rows], as_.at[1], ar.at[1], partner).wait_recv()
-
-    remote(att.at[0], att_out.at[low_rows], as_.at[0], ar.at[0], partner).wait_recv()
-    give.wait()
+        att_near.wait_send()
+        remote(att.at[0], att_out.at[64:128], as_.at[0], ar.at[1], next_chip).wait_recv()
+
+    remote(att.at[0], att_out.at[low_rows], as_.at[0], ar.at[0], next_chip).wait_recv()
+    g_swap[1].wait_recv()
     grad_out[1 - h] = grecv[...].astype(F32)
 
 
@@ -468,17 +556,25 @@
             pltpu.VMEM((2, 8, 2, 4, 128, 256), BF),
             pltpu.VMEM((2, 8, 2, 4, 16, 256), BF),
             pltpu.VMEM((2, 4, 8, 2, 16, 2048), BF),
-            pltpu.VMEM((8, 64, 1024), BF),
+            pltpu.VMEM((4, 128, 1024), BF),
             pltpu.VMEM((256, 1024), BF),
             pltpu.VMEM((2, 64, 1024), BF),
             pltpu.VMEM((2, 64, 1024), BF),
+            pltpu.VMEM((2, 128, 256), F32),
+            pltpu.VMEM((2, 64, 256), BF),
+            pltpu.VMEM((2, 64, 256), BF),
             pltpu.VMEM((256, 1024), BF),
             pltpu.VMEM((256, 1024), BF),
             pltpu.VMEM((2, 256, 2048), BF),
             pltpu.VMEM((2, 64, 1024), BF),
-            pltpu.VMEM((3, 256, 256), BF),
-            pltpu.VMEM((3, 256, 256), BF),
+            pltpu.VMEM((2, 3, 256, 128), BF),
+            pltpu.VMEM((2, 3, 256, 128), BF),
             pltpu.VMEM((256, 128), BF),
+            pltpu.VMEM((256, 128), BF),
+            pltpu.VMEM((256, 128), BF),
+            pltpu.VMEM((2, 64, 256), BF),
+            pltpu.VMEM((2, 64, 1024), BF),
+            pltpu.VMEM((64, 1024), BF),
             pltpu.VMEM((256, 128), BF),
             dma((10,)),
             dma((3, 2, 8)),
@@ -487,16 +583,16 @@
             dma((3, 4)),
             dma((3, 4)),
             dma((3, 4)),
-            dma((8, 4)),
-            dma((8, 4)),
+            dma((7, 4)),
+            dma((7, 4)),
+            dma((2, 3)),
+            dma((2, 3)),
+            dma((3, 2)),
+            dma((3, 2)),
+            dma((2, 3)),
+            dma((2, 3)),
             dma((3,)),
             dma((3,)),
-            dma((4,)),
-            dma((2, 2)),
-            dma((3,)),
-            dma((3,)),
-            dma((2,)),
-            dma((2,)),
         ],
         compiler_params=pltpu.CompilerParams(
             collective_id=0, has_side_effects=True, vmem_limit_bytes=58 * 1024 * 1024

time: 175 us -> 152 us (0.87)
  the two profiles are of different devices: /device:TPU:1 before, /device:TPU:62 now
where the time goes in v2:
time: 152 us
  Pallas kernels  148 us (97%)
  local copies, waits for them, and re-layouts  2.42 us (2%)
    pallas_call x1, Pallas kernels, on_device(): pl.pallas_call(kernel, out_shape=(jax.ShapeDtypeStruct((128, 1024), BF),...  148 us

profile of v2, /device:TPU:62, one launch (start us, length us, event | category | flops | bytes accessed | tf_op | source)
XLA Modules:
  0.0 151.8 jit_solution(9582871979785925661)
XLA Ops:
  1.3 148.1 %shard_map.122 = (bf16[128,1024]{1,0:T(8,128)(2,1)}, f32[2,256,128]{2,1,0:T(8,128)}) custom-call(s32[1]{0:T(128)S(6)} %copy.15.lens, bf16[128,1024]{1,0:T(8,128)(2,1)} %s.1, bf16[2,256,128]{2,1,0:T(8,128)(2,1)} %n.1, bf16[128,1024]{1,0:T(8,128)(2,1)} %q.1, bf16[128,1024]{1,0:T(8,128)(2,1)} %g.1, bf16[512,128]{1,0:T(8,128)(2,1)} %wk.1, bf16[512,128]{1,0:T(8,128)(2,1)} %wv.1, ...), custom_call_target="tpu_custom_call" | custom-call | tf_op jit(solution)/shard_map/pallas_call | solution.py:547
  149.4 0.0 copy-start
  149.4 1.7 %copy.16 = bf16[128,1024]{1,0:T(8,128)(2,1)} copy(bf16[128,1024]{1,0:T(8,128)(2,1)} %get-tuple-element.4) | data formatting | bytes 524288
  151.1 0.0 copy-done
  151.1 0.7 copy.17
Async XLA Ops:
  149.4 1.7 %copy-start = (f32[2,256,128]{2,1,0:T(8,128)S(1)}, f32[2,256,128]{2,1,0:T(8,128)}, u32[]{:S(2)}) copy-start(f32[2,256,128]{2,1,0:T(8,128)} %get-tuple-element.5) | copy-start | bytes 786436

commit v3 on v2

--- a/solution.py
+++ b/solution.py
@@ -69,7 +69,7 @@
     att_out, grad_out,
     we, wqo, wd, sx, nx, qd, gd, kvp, kvs, kvr, mix, prev, gkv, att, part, precv, gsend, grecv,
     n_pass, kv_pass, qg_pass, att_pass, g_pass,
-    lsem, zs, zr, ys, yr, ds, dr, xs, xr, hs, hr, qs, qr, rs, rr, as_, ar,
+    lsem, zs, zr, ys, yr, ds, dr, xs, xr, hs, hr, qs, qr, rs, rr, as_, ar, first_came,
 ):
     y, t, e = lax.axis_index("dp"), lax.axis_index("tensor"), lax.axis_index("enc")
     h, x = lax.div(t, 4), lax.rem(t, 4)
@@ -167,10 +167,10 @@
         greet(along_x(lax.rem(x + k, 4)))
     for k in (1, 3):
         greet(along_y(lax.rem(y + k, 4)))
-    for k in (1, -1):
+    for k in (5, -5, 1, -1):
         greet(along_z(k))
     greet(sibling)
-    pl.semaphore_wait(barrier, 13 + 2 * h)
+    pl.semaphore_wait(barrier, 15 + 2 * h)
 
     def pass_on(k, src, room, dst):
         return (
@@ -200,55 +200,33 @@
     for copy in fetch[:6]:
         copy.wait()
 
-    def y_send(b):
-        def to_both(k):
-            for d, to in ((0, 1), (1, 3)):
-                ref = blocks[k](b, y)
-                remote(ref, ref, ys.at[k, d], yr.at[k, d], along_y(lax.rem(y + to, 4))).start()
-
-        @pl.when(lax.div(b[1], 4) == h)
+    left, right, far = lax.rem(y + 3, 4), lax.rem(y + 1, 4), lax.rem(y + 2, 4)
+
+    def used(b):
+        return pl.when(lax.div(b[1], 4) == h)
+
+    def y_copy(k, d, i, b, yy):
+        ref = blocks[k](b, yy)
+        came = first_came.at[d, i] if k == 0 else yr.at[k, d]
+        return remote(ref, ref, ys.at[k, d], came, along_y(right if d == 0 else left))
+
+    def y_send(k, i, b):
+        def to_both():
+            for d in (0, 1):
+                y_copy(k, d, i, b, y).start()
+
+        if k == 0:
+            used(b)(to_both)
+        else:
+            to_both()
+
+    def y_onward(i, b):
+        @used(b)
         def _():
-            to_both(0)
-
-        to_both(1)
-        to_both(2)
-
-    def z_copy(k, d, step, b):
-        ref = blocks[k](b, y)
-        return remote(ref, ref, zs.at[k, d, step], zr.at[k, d, step], along_z(1 - 2 * d))
-
-    lasts = (8, 7)
-    sent = []
-    for d in (0, 1):
-        for k in kinds:
-            copy = z_copy(k, d, 0, own)
-            copy.start()
-            sent.append(copy)
-    y_send(own)
-
-    for step in range(1, 9):
-        for d in (0, 1):
-            if step > lasts[d]:
-                continue
-            b = z_of(-step if d == 0 else step)
-            for k in kinds:
-                z_copy(k, d, step - 1, b).wait_recv()
-                if step < lasts[d]:
-                    copy = z_copy(k, d, step, b)
-                    copy.start()
-                    sent.append(copy)
-            y_send(b)
-        if step == 1:
-            n_swap[0].wait_recv()
-            n_swap[1].start()
-            n_own.middle()
-        if step == 3:
-            s_ring.middle()
-        if step == 6:
-            n_swap[1].wait_recv()
-            n_other.start()
-
-    left, right, far = lax.rem(y + 3, 4), lax.rem(y + 1, 4), lax.rem(y + 2, 4)
+            for d, yy in ((0, left), (1, right)):
+                y_copy(0, d, i, b, yy).wait_recv()
+                ref = blocks[0](b, yy).at[:, d * 128 : d * 128 + 128]
+                remote(ref, ref, ys.at[0, 2 + d], yr.at[0, 2 + d], along_y(right if d == 0 else left)).start()
 
     def d_copy(k, i, yy, cc):
         ref = whole[k](yy, cc)
@@ -271,11 +249,6 @@
     def d_finish(k):
         for i, yy in enumerate((y, left, right, far)):
             d_copy(k, i, yy, 1 - c).wait_recv()
-
-    for k in kinds:
-        d_copy(k, 0, y, c).start()
-    for k in kinds:
-        y_middle(k)
 
     q_to, q_from = [], []
     for k, (ref, there) in enumerate(((q, qd), (g, gd))):
@@ -293,13 +266,99 @@
     sends_direct = jnp.logical_or(h == 1, c == 0)
     passes_q = jnp.logical_or(from_h == 1, c == 1)
 
-    y_finish(0)
-    y_finish(1)
+    def q_start(k):
+        @pl.when(sends_far)
+        def _():
+            q_to[k][0].start()
+
+        @pl.when(sends_direct)
+        def _():
+            q_to[k][1].start()
+
+    def q_pass(k):
+        @pl.when(passes_q)
+        def _():
+            q_to[k][0].wait_recv()
+            q_from[k].start()
+
+    lasts = (8, 7)
+    sent = []
+
+    def z_copy(k, d, at, b, hops=1):
+        ref = blocks[k](b, y)
+        return remote(ref, ref, zs.at[k, d, at - 1], zr.at[k, d, at - 1], along_z(hops - 2 * hops * d))
+
+    def z_start(k, d, at, b, hops=1):
+        copy = z_copy(k, d, at, b, hops)
+        copy.start()
+        sent.append(copy)
+
+    def z_take(k, d, at):
+        b = z_of(-at if d == 0 else at)
+        z_copy(k, d, at, b).wait_recv()
+        if at != lasts[d] and (k == 2 or at != 4):
+            z_start(k, d, at + 1, b)
+        return d * 8 + at, b
+
+    for k in (0, 1):
+        for d in (0, 1):
+            z_start(k, d, 1, own)
+        for d in (0, 1):
+            z_start(k, d, 5, own, 5)
+    for d in (0, 1):
+        z_start(2, d, 1, own)
+    for k in (0, 1):
+        y_send(k, 0, own)
+
+    early, late = [(0, own)], [(0, own)]
+    for step in range(1, 9):
+        came = [(d, at) for at in (step, step + 3) for d in (0, 1) if at <= lasts[d]]
+        came = [(d, at) for d, at in came if (at == step and step <= 4) or (at > 4 and at == step + 3)]
+        for k in (0, 1):
+            for d, at in came:
+                i, b = z_take(k, d, at)
+                y_send(k, i, b)
+                if k == 0:
+                    early.append((i, b))
+        for d in (0, 1):
+            if step <= lasts[d]:
+                late.append(z_take(2, d, step))
+        if step == 1:
+            n_swap[0].wait_recv()
+            n_swap[1].start()
+            n_own.middle()
+        if step >= 2:
+            keep = len(came)
+            for i, b in early[: len(early) - keep]:
+                y_onward(i, b)
+            early = early[len(early) - keep :]
+        if step == 3:
+            s_ring.middle()
+        if step == 5:
+            q_start(0)
+        if step == 6:
+            n_swap[1].wait_recv()
+            n_other.start()
+            q_pass(0)
+        if step >= 6:
+            for i, b in late:
+                y_send(2, i, b)
+            late = []
+        if step == 6:
+            for i, yy in enumerate((y, left, right)):
+                d_copy(0, i, yy, c).start()
+            d_copy(1, 0, y, c).start()
+            y_middle(1)
+        if step == 7:
+            y_finish(0)
+
+    d_copy(2, 0, y, c).start()
     n_other.middle()
     for copy in fetch[6:]:
         copy.wait()
     for ring in (s_ring, n_own):
         ring.finish()
+    y_finish(1)
     d_finish(0)
 
     for hh in (0, 1):
@@ -314,27 +373,13 @@
     d_finish(1)
     kv_swap[0].wait_recv()
     kv_swap[1].start()
-
-    @pl.when(sends_far)
-    def _():
-        for pair in q_to:
-            pair[0].start()
-
-    @pl.when(sends_direct)
-    def _():
-        for pair in q_to:
-            pair[1].start()
-
+    q_start(1)
     queries = []
     for hh in (0, 1):
         queries.append(dot(nx[...], wqo[hh, :, :, :, :, 0:128].reshape(1024, 128)).astype(BF))
 
-    @pl.when(passes_q)
-    def _():
-        for k in (0, 1):
-            q_to[k][0].wait_recv()
-            q_from[k].start()
-
+    q_pass(1)
+    y_middle(2)
     kv_swap[1].wait_recv()
     first = lax.broadcasted_iota(jnp.int32, (64, 128), 1) < 64
     mix_rings = []
@@ -391,16 +436,16 @@
     live = jnp.logical_and(position < lens[0], position >= 64)
     scale = 1.0 / math.sqrt(128)
 
-    def heads(turn, carry):
-        hh, base = lax.rem(1 - h + lax.div(turn, 2), 2), lax.rem(turn, 2) * 512
+    def heads(turn):
+        hh, base = (1 - h if turn < 2 else h), turn % 2 * 512
         source = prev[...]
-        at_key = pl.ds(pl.multiple_of(base, 512), 512)
-        at_value = pl.ds(pl.multiple_of(1024 + base, 512), 512)
+        at_key = slice(base, base + 512)
+        at_value = slice(1024 + base, 1536 + base)
         keys = dot(source, wd[hh, :, :, :, :, at_key].reshape(1024, 512)).astype(BF)
         values = dot(source, wd[hh, :, :, :, :, at_value].reshape(1024, 512)).astype(BF)
         for a in range(4):
-            at = pl.ds(pl.multiple_of(base + a * 128, 128), 128)
-            later = pl.ds(pl.multiple_of(1024 + base + a * 128, 128), 128)
+            at = slice(base + a * 128, base + a * 128 + 128)
+            later = slice(1024 + base + a * 128, 1152 + base + a * 128)
             key, value = keys[:, a * 128 : a * 128 + 128], values[:, a * 128 : a * 128 + 128]
             query = qd[hh, :, at]
             score = dot(query, key, NT) * scale
@@ -414,35 +459,52 @@
             inner = jnp.sum(slope * probs, axis=-1, keepdims=True)
             slope = (probs * (slope - inner) * scale).astype(BF)
             gkv[hh, :, at] = dot(slope, query, TN).astype(BF)
-        return carry
-
-    lax.fori_loop(0, 2, heads, 0)
 
     low_rows = pl.ds(0, 64)
-    att_far = remote(att.at[1 - h], att_pass, as_.at[0], ar.at[2], next_chip)
-    att_direct = remote(att.at[0], att_out.at[low_rows], as_.at[0], ar.at[0], (y, x, after))
-    att_near = remote(att.at[1], att_out.at[low_rows], as_.at[1], ar.at[0], (y, 4 + x, after))
-    att_on = remote(
-        att_pass, att_out.at[pl.ds(pl.multiple_of((1 - from_h) * 64, 64), 64)], as_.at[2], ar.at[1 - from_h],
-        (y, (1 - from_h) * 4 + x, lax.rem(from_e + from_h, 16)),
-    )
+    on_rows = pl.ds(pl.multiple_of((1 - from_h) * 64, 64), 64)
+    on_device_id = (y, (1 - from_h) * 4 + x, lax.rem(from_e + from_h, 16))
+    att_far, att_direct, att_on = [], [], []
+    for k in (0, 1):
+        part_of = slice(k * 512, k * 512 + 512)
+        att_far.append(
+            remote(att.at[1 - h, :, part_of], att_pass.at[:, part_of], as_.at[k], ar.at[2 + k], next_chip)
+        )
+        att_direct.append(
+            remote(att.at[0, :, part_of], att_out.at[low_rows, part_of], as_.at[k], ar.at[0], (y, x, after))
+        )
+        att_on.append(
+            remote(
+                att_pass.at[:, part_of], att_out.at[on_rows, part_of], as_.at[2 + k], ar.at[1 - from_h],
+                on_device_id,
+            )
+        )
+    att_near = remote(att.at[1], att_out.at[low_rows], as_.at[4], ar.at[0], (y, 4 + x, after))
     direct = jnp.logical_and(h == 1, c == 1)
     passes_att = jnp.logical_or(from_h == 0, c == 0)
 
-    @pl.when(direct)
-    def _():
-        att_direct.start()
-
-    @pl.when(jnp.logical_not(direct))
-    def _():
-        att_far.start()
-
-    lax.fori_loop(2, 4, heads, 0)
-
-    @pl.when(passes_att)
-    def _():
-        att_far.wait_recv()
-        att_on.start()
+    def att_start(k):
+        @pl.when(direct)
+        def _():
+            att_direct[k].start()
+
+        @pl.when(jnp.logical_not(direct))
+        def _():
+            att_far[k].start()
+
+    def att_pass_on(k):
+        @pl.when(passes_att)
+        def _():
+            att_far[k].wait_recv()
+            att_on[k].start()
+
+    heads(0)
+    att_start(0)
+    heads(1)
+    att_start(1)
+    att_pass_on(0)
+    heads(2)
+    att_pass_on(1)
+    heads(3)
 
     @pl.when(h == 0)
     def _():
@@ -520,15 +582,18 @@
 
     @pl.when(direct)
     def _():
-        att_direct.wait_send()
+        for copy in att_direct:
+            copy.wait_send()
 
     @pl.when(jnp.logical_not(direct))
     def _():
-        att_far.wait_send()
+        for copy in att_far:
+            copy.wait_send()
 
     @pl.when(passes_att)
     def _():
-        att_on.wait_send()
+        for copy in att_on:
+            copy.wait_send()
 
     @pl.when(h == 1)
     def _():
@@ -591,8 +656,9 @@
             dma((3, 2)),
             dma((2, 3)),
             dma((2, 3)),
-            dma((3,)),
-            dma((3,)),
+            dma((5,)),
+            dma((4,)),
+            dma((2, 16)),
         ],
         compiler_params=pltpu.CompilerParams(
             collective_id=0, has_side_effects=True, vmem_limit_bytes=58 * 1024 * 1024

time: 152 us -> 154 us (1.013)
  the two profiles are of different devices: /device:TPU:62 before, /device:TPU:50 now
where the time goes in v3:
time: 154 us
  Pallas kernels  150 us (97%)
  local copies, waits for them, and re-layouts  2.42 us (2%)
    pallas_call x1, Pallas kernels, on_device(): pl.pallas_call(kernel, out_shape=(jax.ShapeDtypeStruct((128, 1024), BF),...  150 us

profile of v3, /device:TPU:50, one launch (start us, length us, event | category | flops | bytes accessed | tf_op | source)
XLA Modules:
  0.0 154.1 jit_solution(17197137634456845859)
XLA Ops:
  1.3 150.4 %shard_map.122 = (bf16[128,1024]{1,0:T(8,128)(2,1)}, f32[2,256,128]{2,1,0:T(8,128)}) custom-call(s32[1]{0:T(128)S(6)} %copy.15.lens, bf16[128,1024]{1,0:T(8,128)(2,1)} %s.1, bf16[2,256,128]{2,1,0:T(8,128)(2,1)} %n.1, bf16[128,1024]{1,0:T(8,128)(2,1)} %q.1, bf16[128,1024]{1,0:T(8,128)(2,1)} %g.1, bf16[512,128]{1,0:T(8,128)(2,1)} %wk.1, bf16[512,128]{1,0:T(8,128)(2,1)} %wv.1, ...), custom_call_target="tpu_custom_call" | custom-call | tf_op jit(solution)/shard_map/pallas_call | solution.py:612
  151.7 0.0 copy-start
  151.7 1.7 %copy.16 = bf16[128,1024]{1,0:T(8,128)(2,1)} copy(bf16[128,1024]{1,0:T(8,128)(2,1)} %get-tuple-element.4) | data formatting | bytes 524288
  153.4 0.0 copy-done
  153.4 0.7 copy.17
Async XLA Ops:
  151.7 1.7 %copy-start = (f32[2,256,128]{2,1,0:T(8,128)S(1)}, f32[2,256,128]{2,1,0:T(8,128)}, u32[]{:S(2)}) copy-start(f32[2,256,128]{2,1,0:T(8,128)} %get-tuple-element.5) | copy-start | bytes 786436

commit v4 on v3

--- a/solution.py
+++ b/solution.py
@@ -67,7 +67,7 @@
 def kernel(
     lens, s, n, q, g, wk, wv, wq, wo, wkd, wvd,
     att_out, grad_out,
-    we, wqo, wd, sx, nx, qd, gd, kvp, kvs, kvr, mix, prev, gkv, att, part, precv, gsend, grecv,
+    we, wqo, wd, sx, nx, qd, gd, kvp, kvs, kvr, mix, prev, gkv, att, part, precv, gsum, gsend, grecv,
     n_pass, kv_pass, qg_pass, att_pass, g_pass,
     lsem, zs, zr, ys, yr, ds, dr, xs, xr, hs, hr, qs, qr, rs, rr, as_, ar, first_came,
 ):
@@ -288,14 +288,25 @@
         ref = blocks[k](b, y)
         return remote(ref, ref, zs.at[k, d, at - 1], zr.at[k, d, at - 1], along_z(hops - 2 * hops * d))
 
+    def wanted(k, d, at, b):
+        if k != 0:
+            return lambda body: body()
+        end = 4 if at <= 4 else lasts[d]
+        goal, some = lax.div(b[1], 4), False
+        for reach in range(at, end + 1):
+            there = lax.rem(b[0] * 8 + b[1] + (reach if d == 0 else 16 - reach), 16)
+            some = jnp.logical_or(some, lax.div(there, 8) == goal)
+        return pl.when(some)
+
     def z_start(k, d, at, b, hops=1):
         copy = z_copy(k, d, at, b, hops)
-        copy.start()
-        sent.append(copy)
+        when = wanted(k, d, at, b)
+        when(lambda: copy.start())
+        sent.append((when, copy))
 
     def z_take(k, d, at):
         b = z_of(-at if d == 0 else at)
-        z_copy(k, d, at, b).wait_recv()
+        wanted(k, d, at, b)(lambda: z_copy(k, d, at, b).wait_recv())
         if at != lasts[d] and (k == 2 or at != 4):
             z_start(k, d, at + 1, b)
         return d * 8 + at, b
@@ -311,7 +322,7 @@
         y_send(k, 0, own)
 
     early, late = [(0, own)], [(0, own)]
-    for step in range(1, 9):
+    for step in range(1, 7):
         came = [(d, at) for at in (step, step + 3) for d in (0, 1) if at <= lasts[d]]
         came = [(d, at) for d, at in came if (at == step and step <= 4) or (at > 4 and at == step + 3)]
         for k in (0, 1):
@@ -320,8 +331,8 @@
                 y_send(k, i, b)
                 if k == 0:
                     early.append((i, b))
-        for d in (0, 1):
-            if step <= lasts[d]:
+        if step <= 6:
+            for d in (0, 1):
                 late.append(z_take(2, d, step))
         if step == 1:
             n_swap[0].wait_recv()
@@ -334,31 +345,29 @@
             early = early[len(early) - keep :]
         if step == 3:
             s_ring.middle()
+        if 2 <= step <= 5:
+            for i, b in late[:-2]:
+                y_send(2, i, b)
+            late = late[-2:]
+        if step == 4:
+            q_start(0)
         if step == 5:
-            q_start(0)
-        if step == 6:
             n_swap[1].wait_recv()
             n_other.start()
             q_pass(0)
-        if step >= 6:
-            for i, b in late:
-                y_send(2, i, b)
-            late = []
         if step == 6:
             for i, yy in enumerate((y, left, right)):
                 d_copy(0, i, yy, c).start()
             d_copy(1, 0, y, c).start()
             y_middle(1)
-        if step == 7:
+            for i, b in late:
+                y_send(2, i, b)
+            n_other.middle()
             y_finish(0)
 
-    d_copy(2, 0, y, c).start()
-    n_other.middle()
     for copy in fetch[6:]:
         copy.wait()
-    for ring in (s_ring, n_own):
-        ring.finish()
-    y_finish(1)
+    s_ring.finish()
     d_finish(0)
 
     for hh in (0, 1):
@@ -369,17 +378,22 @@
         kvs[hh] = kvp[hh, far_rows].astype(BF)
     kv_swap = pass_on(1, kvs, kv_pass, kvr)
     kv_swap[0].start()
-    n_other.finish()
-    d_finish(1)
+    y_finish(1)
+    for d in (0, 1):
+        i, b = z_take(2, d, 7)
+        y_send(2, i, b)
+    n_own.finish()
     kv_swap[0].wait_recv()
     kv_swap[1].start()
     q_start(1)
+    i, b = z_take(2, 0, 8)
+    y_send(2, i, b)
+    d_copy(2, 0, y, c).start()
+    d_finish(1)
+    n_other.finish()
     queries = []
     for hh in (0, 1):
         queries.append(dot(nx[...], wqo[hh, :, :, :, :, 0:128].reshape(1024, 128)).astype(BF))
-
-    q_pass(1)
-    y_middle(2)
     kv_swap[1].wait_recv()
     first = lax.broadcasted_iota(jnp.int32, (64, 128), 1) < 64
     mix_rings = []
@@ -397,9 +411,10 @@
         ring = wide_ring(mix, hh, 3 + hh)
         ring.start()
         mix_rings.append(ring)
+    y_middle(2)
     for ring in mix_rings:
         ring.middle()
-    y_finish(2)
+    q_pass(1)
     for ring in mix_rings:
         ring.finish()
     prev_rings = []
@@ -414,6 +429,7 @@
         ring.middle()
     for ring in prev_rings:
         ring.finish()
+    y_finish(2)
     d_finish(2)
 
     def q_wait(slot):
@@ -454,11 +470,11 @@
             low = probs.astype(BF)
             att[hh, :, at] = jnp.where(live, dot(low, value), 0.0).astype(BF)
             cot = jnp.where(live, gd[hh, :, at].astype(F32), 0.0).astype(BF)
-            gkv[hh, :, later] = dot(low, cot, TN).astype(BF)
+            gkv[hh, later, :] = dot(cot, low, TN).astype(BF)
             slope = dot(cot, value, NT)
             inner = jnp.sum(slope * probs, axis=-1, keepdims=True)
             slope = (probs * (slope - inner) * scale).astype(BF)
-            gkv[hh, :, at] = dot(slope, query, TN).astype(BF)
+            gkv[hh, at, :] = dot(query, slope, TN).astype(BF)
 
     low_rows = pl.ds(0, 64)
     on_rows = pl.ds(pl.multiple_of((1 - from_h) * 64, 64), 64)
@@ -501,10 +517,10 @@
     att_start(0)
     heads(1)
     att_start(1)
+    heads(2)
     att_pass_on(0)
-    heads(2)
+    heads(3)
     att_pass_on(1)
-    heads(3)
 
     @pl.when(h == 0)
     def _():
@@ -514,42 +530,45 @@
     def _():
         att_near.start()
 
-    def share(k, to):
-        total = jnp.zeros((256, 128), F32)
+    def share(to):
+        total = jnp.zeros((256, 256), F32)
         for hh in (0, 1):
-            rows = wd[hh, lax.div(k * 4 + to, 2), pl.ds(lax.rem(to, 2) * 4, 4)].reshape(128, 2048)
-            total = total + dot(gkv[hh], rows, NT)
+            rows = [
+                wd[hh, lax.div(k * 4 + to, 2), pl.ds(lax.rem(to, 2) * 4, 4)].reshape(128, 2048)
+                for k in (0, 1)
+            ]
+            total = total + dot(jnp.concatenate(rows, axis=0), gkv[hh])
         return total
 
     shares = []
-
-    def give_shares(i, k):
-        for m in (2, 1, 3):
-            to = lax.rem(x + m, 4)
-            part[i, m - 1] = share(k, to).astype(BF)
-            copy = remote(part.at[i, m - 1], precv.at[i, m - 1], rs.at[i, m - 1], rr.at[i, m - 1], along_x(to))
-            copy.start()
-            shares.append(copy)
-
-    def take_shares(i, total):
+    for m in (2, 1, 3):
+        to = lax.rem(x + m, 4)
+        part[m - 1] = share(to).astype(BF)
+        copy = remote(part.at[m - 1], precv.at[m - 1], rs.at[m - 1], rr.at[m - 1], along_x(to))
+        copy.start()
+        shares.append(copy)
+    gsum[...] = share(x)
+    for m in (2, 1, 3):
+        remote(part.at[m - 1], precv.at[m - 1], rs.at[m - 1], rr.at[m - 1], next_chip).wait_recv()
+    near_cols = pl.ds(pl.multiple_of(h * 128, 128), 128)
+    far_cols = pl.ds(pl.multiple_of((1 - h) * 128, 128), 128)
+
+    def summed(cols):
+        total = gsum[cols]
         for m in (1, 3, 2):
-            remote(
-                part.at[i, m - 1], precv.at[i, m - 1], rs.at[i, m - 1], rr.at[i, m - 1], next_chip
-            ).wait_recv()
-            total = total + precv[i, m - 1].astype(F32)
+            total = total + precv[m - 1, cols].astype(F32)
         return total
 
-    give_shares(0, 1 - h)
-    total = share(1 - h, x)
-    gsend[...] = take_shares(0, total).astype(BF)
+    gsend[...] = summed(far_cols).astype(BF)
     g_swap = pass_on(2, gsend, g_pass, grecv)
     g_swap[0].start()
-    give_shares(1, h)
+    grad_out[h] = summed(near_cols).T
     g_swap[0].wait_recv()
     g_swap[1].start()
-    grad_out[h] = take_shares(1, share(h, x))
-
-    for copy in sent + shares:
+
+    for when, copy in sent:
+        when(copy.wait_send)
+    for copy in shares:
         copy.wait_send()
     for pair in (n_swap, kv_swap, g_swap):
         for copy in pair:
@@ -602,7 +621,7 @@
 
     remote(att.at[0], att_out.at[low_rows], as_.at[0], ar.at[0], next_chip).wait_recv()
     g_swap[1].wait_recv()
-    grad_out[1 - h] = grecv[...].astype(F32)
+    grad_out[1 - h] = grecv[...].astype(F32).T
 
 
 def on_device(span_states, neighbours, lengths, wq, wk, wv, wo, wkd, wvd, queries, grad_out):
@@ -630,17 +649,18 @@
             pltpu.VMEM((2, 64, 256), BF),
             pltpu.VMEM((256, 1024), BF),
             pltpu.VMEM((256, 1024), BF),
-            pltpu.VMEM((2, 256, 2048), BF),
+            pltpu.VMEM((2, 2048, 256), BF),
             pltpu.VMEM((2, 64, 1024), BF),
-            pltpu.VMEM((2, 3, 256, 128), BF),
-            pltpu.VMEM((2, 3, 256, 128), BF),
-            pltpu.VMEM((256, 128), BF),
-            pltpu.VMEM((256, 128), BF),
+            pltpu.VMEM((3, 256, 256), BF),
+            pltpu.VMEM((3, 256, 256), BF),
+            pltpu.VMEM((256, 256), F32),
+            pltpu.VMEM((128, 256), BF),
+            pltpu.VMEM((128, 256), BF),
             pltpu.VMEM((256, 128), BF),
             pltpu.VMEM((2, 64, 256), BF),
             pltpu.VMEM((2, 64, 1024), BF),
             pltpu.VMEM((64, 1024), BF),
-            pltpu.VMEM((256, 128), BF),
+            pltpu.VMEM((128, 256), BF),
             dma((10,)),
             dma((3, 2, 8)),
             dma((3, 2, 8)),
@@ -654,8 +674,8 @@
             dma((2, 3)),
             dma((3, 2)),
             dma((3, 2)),
-            dma((2, 3)),
-            dma((2, 3)),
+            dma((3,)),
+            dma((3,)),
             dma((5,)),
             dma((4,)),
             dma((2, 16)),

time: 154 us -> 137 us (0.89)
  the two profiles are of different devices: /device:TPU:50 before, /device:TPU:160 now
where the time goes in v4:
time: 137 us
  Pallas kernels  133 us (97%)
  local copies, waits for them, and re-layouts  2.42 us (2%)
    pallas_call x1, Pallas kernels, on_device(): pl.pallas_call(kernel, out_shape=(jax.ShapeDtypeStruct((128, 1024), BF),...  133 us

profile of v4, /device:TPU:160, one launch (start us, length us, event | category | flops | bytes accessed | tf_op | source)
XLA Modules:
  0.0 136.9 jit_solution(1184504993454276828)
XLA Ops:
  1.3 133.2 %shard_map.122 = (bf16[128,1024]{1,0:T(8,128)(2,1)}, f32[2,256,128]{2,1,0:T(8,128)}) custom-call(s32[1]{0:T(128)S(6)} %copy.15.lens, bf16[128,1024]{1,0:T(8,128)(2,1)} %s.1, bf16[2,256,128]{2,1,0:T(8,128)(2,1)} %n.1, bf16[128,1024]{1,0:T(8,128)(2,1)} %q.1, bf16[128,1024]{1,0:T(8,128)(2,1)} %g.1, bf16[512,128]{1,0:T(8,128)(2,1)} %wk.1, bf16[512,128]{1,0:T(8,128)(2,1)} %wv.1, ...), custom_call_target="tpu_custom_call" | custom-call | tf_op jit(solution)/shard_map/pallas_call | solution.py:631
  134.4 0.0 copy-start
  134.4 1.7 %copy.16 = bf16[128,1024]{1,0:T(8,128)(2,1)} copy(bf16[128,1024]{1,0:T(8,128)(2,1)} %get-tuple-element.4) | data formatting | bytes 524288
  136.2 0.0 copy-done
  136.2 0.7 copy.17
Async XLA Ops:
  134.4 1.7 %copy-start = (f32[2,256,128]{2,1,0:T(8,128)S(1)}, f32[2,256,128]{2,1,0:T(8,128)}, u32[]{:S(2)}) copy-start(f32[2,256,128]{2,1,0:T(8,128)} %get-tuple-element.5) | copy-start | bytes 786436

commit v5 on v4

--- a/solution.py
+++ b/solution.py
@@ -207,7 +207,7 @@
 
     def y_copy(k, d, i, b, yy):
         ref = blocks[k](b, yy)
-        came = first_came.at[d, i] if k == 0 else yr.at[k, d]
+        came = yr.at[k, d] if k == 1 else first_came.at[k // 2, d, i]
         return remote(ref, ref, ys.at[k, d], came, along_y(right if d == 0 else left))
 
     def y_send(k, i, b):
@@ -220,13 +220,19 @@
         else:
             to_both()
 
-    def y_onward(i, b):
-        @used(b)
-        def _():
+    def y_onward(k, i, b):
+        def onward():
             for d, yy in ((0, left), (1, right)):
-                y_copy(0, d, i, b, yy).wait_recv()
-                ref = blocks[0](b, yy).at[:, d * 128 : d * 128 + 128]
-                remote(ref, ref, ys.at[0, 2 + d], yr.at[0, 2 + d], along_y(right if d == 0 else left)).start()
+                y_copy(k, d, i, b, yy).wait_recv()
+                ref = blocks[k](b, yy)
+                width = ref.shape[-1] // 2
+                ref = ref.at[:, d * width : d * width + width]
+                remote(ref, ref, ys.at[k, 2 + d], yr.at[k, 2 + d], along_y(right if d == 0 else left)).start()
+
+        if k == 0:
+            used(b)(onward)
+        else:
+            onward()
 
     def d_copy(k, i, yy, cc):
         ref = whole[k](yy, cc)
@@ -321,7 +327,7 @@
     for k in (0, 1):
         y_send(k, 0, own)
 
-    early, late = [(0, own)], [(0, own)]
+    early, late, gone = [(0, own)], [(0, own)], []
     for step in range(1, 7):
         came = [(d, at) for at in (step, step + 3) for d in (0, 1) if at <= lasts[d]]
         came = [(d, at) for d, at in came if (at == step and step <= 4) or (at > 4 and at == step + 3)]
@@ -331,7 +337,7 @@
                 y_send(k, i, b)
                 if k == 0:
                     early.append((i, b))
-        if step <= 6:
+        if step <= 5:
             for d in (0, 1):
                 late.append(z_take(2, d, step))
         if step == 1:
@@ -341,14 +347,14 @@
         if step >= 2:
             keep = len(came)
             for i, b in early[: len(early) - keep]:
-                y_onward(i, b)
+                y_onward(0, i, b)
             early = early[len(early) - keep :]
         if step == 3:
             s_ring.middle()
         if 2 <= step <= 5:
             for i, b in late[:-2]:
                 y_send(2, i, b)
-            late = late[-2:]
+            gone, late = gone + late[:-2], late[-2:]
         if step == 4:
             q_start(0)
         if step == 5:
@@ -360,8 +366,10 @@
                 d_copy(0, i, yy, c).start()
             d_copy(1, 0, y, c).start()
             y_middle(1)
+            late = late + [z_take(2, d, step) for d in (0, 1)]
             for i, b in late:
                 y_send(2, i, b)
+            gone = gone + late
             n_other.middle()
             y_finish(0)
 
@@ -378,23 +386,30 @@
         kvs[hh] = kvp[hh, far_rows].astype(BF)
     kv_swap = pass_on(1, kvs, kv_pass, kvr)
     kv_swap[0].start()
+
+    def late_step(step):
+        took = [z_take(2, d, step) for d in (0, 1) if step <= lasts[d]]
+        for i, b in took:
+            y_send(2, i, b)
+        return took
+
     y_finish(1)
-    for d in (0, 1):
-        i, b = z_take(2, d, 7)
-        y_send(2, i, b)
+    last_gone = late_step(7)
     n_own.finish()
     kv_swap[0].wait_recv()
     kv_swap[1].start()
     q_start(1)
-    i, b = z_take(2, 0, 8)
-    y_send(2, i, b)
+    last_gone = last_gone + late_step(8)
     d_copy(2, 0, y, c).start()
     d_finish(1)
     n_other.finish()
     queries = []
     for hh in (0, 1):
         queries.append(dot(nx[...], wqo[hh, :, :, :, :, 0:128].reshape(1024, 128)).astype(BF))
+    for i, b in gone:
+        y_onward(2, i, b)
     kv_swap[1].wait_recv()
+    q_pass(1)
     first = lax.broadcasted_iota(jnp.int32, (64, 128), 1) < 64
     mix_rings = []
     for hh in (0, 1):
@@ -411,10 +426,12 @@
         ring = wide_ring(mix, hh, 3 + hh)
         ring.start()
         mix_rings.append(ring)
-    y_middle(2)
+    for i, b in last_gone:
+        y_onward(2, i, b)
+    for i, yy in ((1, left), (2, right)):
+        d_copy(2, i, yy, c).start()
     for ring in mix_rings:
         ring.middle()
-    q_pass(1)
     for ring in mix_rings:
         ring.finish()
     prev_rings = []
@@ -425,11 +442,11 @@
         ring = wide_ring(prev, hh, 5 + hh)
         ring.start()
         prev_rings.append(ring)
+    y_finish(2)
     for ring in prev_rings:
         ring.middle()
     for ring in prev_rings:
         ring.finish()
-    y_finish(2)
     d_finish(2)
 
     def q_wait(slot):
@@ -678,7 +695,7 @@
             dma((3,)),
             dma((5,)),
             dma((4,)),
-            dma((2, 16)),
+            dma((2, 2, 16)),
         ],
         compiler_params=pltpu.CompilerParams(
             collective_id=0, has_side_effects=True, vmem_limit_bytes=58 * 1024 * 1024

time: 137 us -> 137 us (level)
  the two profiles are of different devices: /device:TPU:160 before, /device:TPU:100 now
where the time goes in v5:
time: 137 us
  Pallas kernels  134 us (98%)
  local copies, waits for them, and re-layouts  2.42 us (2%)
    pallas_call x1, Pallas kernels, on_device(): pl.pallas_call(kernel, out_shape=(jax.ShapeDtypeStruct((128, 1024), BF),...  134 us

profile of v5, /device:TPU:100, one launch (start us, length us, event | category | flops | bytes accessed | tf_op | source)
XLA Modules:
  0.0 137.3 jit_solution(9814381299400020449)
XLA Ops:
  1.3 133.6 %shard_map.122 = (bf16[128,1024]{1,0:T(8,128)(2,1)}, f32[2,256,128]{2,1,0:T(8,128)}) custom-call(s32[1]{0:T(128)S(6)} %copy.15.lens, bf16[128,1024]{1,0:T(8,128)(2,1)} %s.1, bf16[2,256,128]{2,1,0:T(8,128)(2,1)} %n.1, bf16[128,1024]{1,0:T(8,128)(2,1)} %q.1, bf16[128,1024]{1,0:T(8,128)(2,1)} %g.1, bf16[512,128]{1,0:T(8,128)(2,1)} %wk.1, bf16[512,128]{1,0:T(8,128)(2,1)} %wv.1, ...), custom_call_target="tpu_custom_call" | custom-call | tf_op jit(solution)/shard_map/pallas_call | solution.py:648
  134.9 0.0 copy-start
  134.9 1.7 %copy.16 = bf16[128,1024]{1,0:T(8,128)(2,1)} copy(bf16[128,1024]{1,0:T(8,128)(2,1)} %get-tuple-element.4) | data formatting | bytes 524288
  136.6 0.0 copy-done
  136.6 0.7 copy.17
Async XLA Ops:
  134.9 1.7 %copy-start = (f32[2,256,128]{2,1,0:T(8,128)S(1)}, f32[2,256,128]{2,1,0:T(8,128)}, u32[]{:S(2)}) copy-start(f32[2,256,128]{2,1,0:T(8,128)} %get-tuple-element.5) | copy-start | bytes 786436

commit v6 on v5

--- a/solution.py
+++ b/solution.py
@@ -102,6 +102,10 @@
     onto = along_z(8 - way)
     from_h, from_j = z_of(-way)
     from_e = from_j * 2 + c
+    out_chip = along_z(7 * way)
+    out_onto = along_z(way)
+    out_h, out_j = z_of(-7 * way)
+    out_e = out_j * 2 + c
 
     use = pl.ds(h * 4, 4)
     blocks = (
@@ -167,15 +171,17 @@
         greet(along_x(lax.rem(x + k, 4)))
     for k in (1, 3):
         greet(along_y(lax.rem(y + k, 4)))
+    for k in (1, -1):
+        greet(along_z(k, 1 - c))
     for k in (5, -5, 1, -1):
         greet(along_z(k))
     greet(sibling)
-    pl.semaphore_wait(barrier, 15 + 2 * h)
-
-    def pass_on(k, src, room, dst):
+    pl.semaphore_wait(barrier, 17 + 2 * h)
+
+    def pass_on(k, src, room, dst, relay=next_chip, end=onto):
         return (
-            remote(src, room, hs.at[0, k], hr.at[0, k], next_chip),
-            remote(room, dst, hs.at[1, k], hr.at[1, k], onto),
+            remote(src, room, hs.at[0, k], hr.at[0, k], relay),
+            remote(room, dst, hs.at[1, k], hr.at[1, k], end),
         )
 
     n_swap = pass_on(0, n.at[1 - h], n_pass, nx.at[:, lanes(from_h * 4 + x, 128)])
@@ -494,26 +500,26 @@
             gkv[hh, at, :] = dot(query, slope, TN).astype(BF)
 
     low_rows = pl.ds(0, 64)
-    on_rows = pl.ds(pl.multiple_of((1 - from_h) * 64, 64), 64)
-    on_device_id = (y, (1 - from_h) * 4 + x, lax.rem(from_e + from_h, 16))
+    on_rows = pl.ds(pl.multiple_of((1 - out_h) * 64, 64), 64)
+    on_device_id = (y, (1 - out_h) * 4 + x, lax.rem(out_e + out_h, 16))
     att_far, att_direct, att_on = [], [], []
     for k in (0, 1):
         part_of = slice(k * 512, k * 512 + 512)
         att_far.append(
-            remote(att.at[1 - h, :, part_of], att_pass.at[:, part_of], as_.at[k], ar.at[2 + k], next_chip)
+            remote(att.at[1 - h, :, part_of], att_pass.at[:, part_of], as_.at[k], ar.at[2 + k], out_chip)
         )
         att_direct.append(
             remote(att.at[0, :, part_of], att_out.at[low_rows, part_of], as_.at[k], ar.at[0], (y, x, after))
         )
         att_on.append(
             remote(
-                att_pass.at[:, part_of], att_out.at[on_rows, part_of], as_.at[2 + k], ar.at[1 - from_h],
+                att_pass.at[:, part_of], att_out.at[on_rows, part_of], as_.at[2 + k], ar.at[1 - out_h],
                 on_device_id,
             )
         )
     att_near = remote(att.at[1], att_out.at[low_rows], as_.at[4], ar.at[0], (y, 4 + x, after))
     direct = jnp.logical_and(h == 1, c == 1)
-    passes_att = jnp.logical_or(from_h == 0, c == 0)
+    passes_att = jnp.logical_or(out_h == 0, c == 0)
 
     def att_start(k):
         @pl.when(direct)
@@ -535,9 +541,7 @@
     heads(1)
     att_start(1)
     heads(2)
-    att_pass_on(0)
     heads(3)
-    att_pass_on(1)
 
     @pl.when(h == 0)
     def _():
@@ -565,6 +569,8 @@
         copy.start()
         shares.append(copy)
     gsum[...] = share(x)
+    att_pass_on(0)
+    att_pass_on(1)
     for m in (2, 1, 3):
         remote(part.at[m - 1], precv.at[m - 1], rs.at[m - 1], rr.at[m - 1], next_chip).wait_recv()
     near_cols = pl.ds(pl.multiple_of(h * 128, 128), 128)
@@ -577,7 +583,7 @@
         return total
 
     gsend[...] = summed(far_cols).astype(BF)
-    g_swap = pass_on(2, gsend, g_pass, grecv)
+    g_swap = pass_on(2, gsend, g_pass, grecv, out_chip, out_onto)
     g_swap[0].start()
     grad_out[h] = summed(near_cols).T
     g_swap[0].wait_recv()

time: 137 us -> 134 us (0.978)
  the two profiles are of different devices: /device:TPU:100 before, /device:TPU:128 now
where the time goes in v6:
time: 134 us
  Pallas kernels  130 us (97%)
  local copies, waits for them, and re-layouts  2.42 us (2%)
    pallas_call x1, Pallas kernels, on_device(): pl.pallas_call(kernel, out_shape=(jax.ShapeDtypeStruct((128, 1024), BF),...  130 us

profile of v6, /device:TPU:128, one launch (start us, length us, event | category | flops | bytes accessed | tf_op | source)
XLA Modules:
  0.0 134.0 jit_solution(7324042120472044186)
XLA Ops:
  1.3 130.3 %shard_map.122 = (bf16[128,1024]{1,0:T(8,128)(2,1)}, f32[2,256,128]{2,1,0:T(8,128)}) custom-call(s32[1]{0:T(128)S(6)} %copy.15.lens, bf16[128,1024]{1,0:T(8,128)(2,1)} %s.1, bf16[2,256,128]{2,1,0:T(8,128)(2,1)} %n.1, bf16[128,1024]{1,0:T(8,128)(2,1)} %q.1, bf16[128,1024]{1,0:T(8,128)(2,1)} %g.1, bf16[512,128]{1,0:T(8,128)(2,1)} %wk.1, bf16[512,128]{1,0:T(8,128)(2,1)} %wv.1, ...), custom_call_target="tpu_custom_call" | custom-call | tf_op jit(solution)/shard_map/pallas_call | solution.py:654
  131.6 0.0 copy-start
  131.6 1.7 %copy.16 = bf16[128,1024]{1,0:T(8,128)(2,1)} copy(bf16[128,1024]{1,0:T(8,128)(2,1)} %get-tuple-element.4) | data formatting | bytes 524288
  133.3 0.0 copy-done
  133.3 0.7 copy.17
Async XLA Ops:
  131.6 1.7 %copy-start = (f32[2,256,128]{2,1,0:T(8,128)S(1)}, f32[2,256,128]{2,1,0:T(8,128)}, u32[]{:S(2)}) copy-start(f32[2,256,128]{2,1,0:T(8,128)} %get-tuple-element.5) | copy-start | bytes 786436
